TPU v7x, 32 devices: a whole 2x2x4 slice. The times are simulated.
32 devices in a mesh: views: 2 (over x), depth: 16 (over z, y, core).
Axes of the slice: x: 2, y: 2, z: 4, core: 2. Of those that a mesh axis runs over, the one named last changes fastest.
Arguments:
- density: float32 [512, 128, 256], P(('views', 'depth')), parts along dimension 0, may hold values from 0.2 to 5
- emission: bfloat16 [6, 256, 128, 256], P('views', 'depth'), parts along dimension 0, may hold values from 0 to 1
- occupancy: int32 [32, 4, 4], P(('views', 'depth')), parts along dimension 0, may hold values 0 or 1
- facing: int32 [2], P('views'), parts along dimension 0, may hold values from 0 to 1
Outputs:
- image: float32 [8, 128, 256], P('views', 'depth'), parts along dimension 0
There are 2 independent parts, one for each index of `views`. A program takes and returns all parts, laid end to end along the dimension named above; each array names one. Nothing has to cross between parts.
Inputs may be any that keep to these rules, and one draw needn't show every extreme that they name: `occupancy`: 1 where the tile of the brick is occupied; where it is 0 the tile's cells neither absorb nor emit. `facing`: 0: bricks and cells of lower depth index are nearer the camera; 1: those of higher index.
All inputs are finite; a program needn't handle non-finite values. No bound on the sum of `occupancy` on one device may be relied on, other than what follows from the above.
Results may differ from a plain program's by a relative error of at most 0.0003.
Values sent between devices are 32-bit elements; how exact they have to be, the bound alone decides.
No kernel may reach another device: no remote copies, remote signals or barrier semaphores. Data moves between devices by JAX's collectives and lax.ppermute only.
A program may use at most 128 MiB of HBM per device.

v0:
```python
import jax
import jax.numpy as jnp
from jax import lax
from jax.sharding import PartitionSpec as P


def march(dense, emitted, occupied, facing, bricks):
    depth_len, height, width = dense.shape
    tiles_h, tiles_w = occupied.shape
    gating = occupied.astype(jnp.float32)[None, :, None, :, None]
    optical = (
        dense.reshape(depth_len, tiles_h, height // tiles_h, tiles_w, width // tiles_w) * gating
    ).reshape(dense.shape) / (depth_len * bricks)
    column = jnp.cumsum(optical, axis=0)
    whole = column[-1]
    ahead = jnp.where(facing == 0, column - optical, whole[None] - column)
    weight = (1.0 - jnp.exp(-optical)) * jnp.exp(-ahead)
    radiance = jnp.sum(emitted.astype(jnp.float32) * weight[None], axis=1)
    return (radiance, jnp.exp(-whole))


def composite(radiance, transmit, facing):
    ones_row = jnp.ones_like(transmit[:1])
    forward = jnp.cumprod(transmit, axis=0)
    ahead_forward = jnp.concatenate([ones_row, forward[:-1]], axis=0)
    backward = jnp.flip(jnp.cumprod(jnp.flip(transmit, 0), axis=0), 0)
    ahead_backward = jnp.concatenate([backward[1:], ones_row], axis=0)
    front = jnp.where(facing == 0, ahead_forward, ahead_backward)
    colour = jnp.sum(radiance * front, axis=0)
    opacity = 1.0 - forward[-1]
    return jnp.concatenate([colour, opacity], axis=0)


def on_device(density, emission, occupancy, facing):
    bricks = lax.axis_size("depth")
    facing_now = facing[0]
    radiance, transmit = march(density, emission, occupancy[0], facing_now, bricks)
    every_colour, every_transmit = (
        lax.all_to_all(radiance[None], "depth", split_axis=2, concat_axis=0, tiled=True),
        lax.all_to_all(transmit[None, None], "depth", split_axis=2, concat_axis=0, tiled=True),
    )
    return composite(every_colour, every_transmit, facing_now)


def solution(mesh):
    return jax.shard_map(
        on_device,
        mesh=mesh,
        in_specs=(
            P(("views", "depth"), None, None),
            P("views", "depth", None, None),
            P(("views", "depth"), None, None),
            P("views"),
        ),
        out_specs=P("views", "depth", None),
        check_vma=False,
    )
```

profile of v0, /device:TPU:0, one launch (start us, length us, event | category | flops | bytes accessed | tf_op | source)
XLA Modules:
  0.0 35.3 jit_solution(3524464965204813712)
XLA Ops:
  0.0 0.7 %convert_bitcast_fusion = f32[4,4]{1,0:T(4,128)S(1)} fusion(s32[1,4,4]{2,1,0:T(4,128)} %param.6), kind=kLoop, calls=%fused_computation.14 | loop fusion | flops 16 | bytes 128 | tf_op jit(solution)/shard_map/convert_element_type | solution.py:10
  0.7 0.1 mul.37
  0.8 0.2 mul.38
  1.0 1.8 %fusion = f32[16,128,256]{2,1,0:T(8,128)S(1)} fusion(f32[16,128,256]{2,1,0:T(8,128)} %param.4, f32[128,256]{1,0:T(8,128)S(1)} %mul.38), kind=kOutput, calls=%fused_computation.3 | output fusion | flops 8912896 | bytes 4325376 | tf_op jit(solution)/shard_map/jit(cumsum)/reduce_window_sum | solution.py:14
  2.8 0.8 %copy.18 = f32[1,1,128,256]{3,1,0,2:T(1,128)} copy(f32[1,1,128,256]{3,2,1,0:T(8,128)S(1)} %get-tuple-element.6) | data formatting | bytes 262144 | tf_op jit(solution)/shard_map/exp | solution.py:19
  3.6 7.4 %all-to-all-start.1 = ((f32[1,1,128,256]{3,1,0,2:T(1,128)}), f32[1,1,128,256]{3,1,0,2:T(1,128)S(1)}, u32[]{:S(2)}, u32[]{:S(2)}) async-start(f32[1,1,128,256]{3,1,0,2:T(1,128)} %copy.18), calls=%async_computation.1 | async-start | bytes 262144 | tf_op jit(solution)/shard_map/all_to_all | solution.py:40
  11.7 0.0 copy-start
  11.7 2.6 %exponential_multiply_fusion = f32[16,128,256]{2,1,0:T(8,128)S(1)} fusion(f32[16,128,256]{2,1,0:T(8,128)S(1)} %fusion, f32[16,128,256]{2,1,0:T(8,128)} %param.4, f32[128,256]{1,0:T(8,128)S(1)} %get-tuple-element.5, f32[128,256]{1,0:T(8,128)S(1)} %mul.38, pred[]{:T(512)} %bitcast.1), kind=kLoop, calls=%fused_computation.1 | loop fusion | flops 4718592 | bytes 6553601 | tf_op jit(solution)/shard_map/mul | solution.py:17
  14.3 0.0 copy-done
  14.3 0.6 %multiply_reduce_fusion = f32[3,128,256]{2,1,0:T(8,128)S(1)} fusion(bf16[3,16,128,256]{3,2,1,0:T(8,128)(2,1)S(1)} %copy-done, f32[16,128,256]{2,1,0:T(8,128)S(1)} %exponential_multiply_fusion), kind=kLoop, calls=%fused_computation | loop fusion | flops 4620288 | bytes 5636096 | tf_op jit(solution)/shard_map/reduce_sum | solution.py:18
  14.9 1.1 %copy.16 = f32[1,3,128,256]{3,0,1,2:T(1,128)} copy(f32[1,3,128,256]{3,2,1,0:T(8,128)S(1)} %bitcast.22) | data formatting | bytes 786432 | tf_op jit(solution)/shard_map/broadcast_in_dim | solution.py:39
  16.1 2.9 %all-to-all-done.1 = f32[1,1,128,256]{3,1,0,2:T(1,128)S(1)} async-done(((f32[1,1,128,256]{3,1,0,2:T(1,128)}), f32[1,1,128,256]{3,1,0,2:T(1,128)S(1)}, u32[]{:S(2)}, u32[]{:S(2)}) %all-to-all-start.1) | async-done | bytes 131104 | tf_op jit(solution)/shard_map/all_to_all | solution.py:40
  18.9 3.6 %all-to-all-start = ((f32[1,3,128,256]{3,0,1,2:T(1,128)}), f32[1,3,128,256]{3,0,1,2:T(1,128)S(1)}, u32[]{:S(2)}, u32[]{:S(2)}) async-start(f32[1,3,128,256]{3,0,1,2:T(1,128)} %copy.16), calls=%async_computation | async-start | bytes 786432 | tf_op jit(solution)/shard_map/all_to_all | solution.py:39
  22.5 1.4 %fusion.8 = f32[16,1,8,256]{3,2,1,0:T(8,128)S(1)} fusion(f32[16,1,8,256]{3,2,1,0:T(8,128)S(1)} %rev.5), kind=kOutput, calls=%fused_computation.18 | output fusion | flops 491520 | bytes 262144 | tf_op jit(solution)/shard_map/jit(cumprod)/reduce_window | solution.py:26
  23.9 0.1 fusion.6
  24.1 10.5 %all-to-all-done = f32[1,3,128,256]{3,0,1,2:T(1,128)S(1)} async-done(((f32[1,3,128,256]{3,0,1,2:T(1,128)}), f32[1,3,128,256]{3,0,1,2:T(1,128)S(1)}, u32[]{:S(2)}, u32[]{:S(2)}) %all-to-all-start) | async-done | bytes 393248 | tf_op jit(solution)/shard_map/all_to_all | solution.py:39
  34.7 0.6 %copy.23 = f32[4,8,256]{2,1,0:T(8,128)} copy(f32[4,8,256]{2,0,1:T(4,128)S(1)} %pad_maximum_fusion) | data formatting | bytes 65536 | tf_op jit(solution)/shard_map/concatenate | solution.py:31
  (12 shorter events, 0.2 us)
Async XLA Ops:
  3.6 15.3 %all-to-all-start.1 = ((f32[1,1,128,256]{3,1,0,2:T(1,128)}), f32[1,1,128,256]{3,1,0,2:T(1,128)S(1)}, u32[]{:S(2)}, u32[]{:S(2)}) async-start(f32[1,1,128,256]{3,1,0,2:T(1,128)} %copy.18), calls=%async_computation.1 | async-start | bytes 262144 | tf_op jit(solution)/shard_map/all_to_all | solution.py:40
  11.7 2.6 %copy-start = (bf16[3,16,128,256]{3,2,1,0:T(8,128)(2,1)S(1)}, bf16[3,16,128,256]{3,2,1,0:T(8,128)(2,1)}, u32[]{:S(2)}) copy-start(bf16[3,16,128,256]{3,2,1,0:T(8,128)(2,1)} %param.5) | copy-start | bytes 9437188
  18.9 15.7 %all-to-all-start = ((f32[1,3,128,256]{3,0,1,2:T(1,128)}), f32[1,3,128,256]{3,0,1,2:T(1,128)S(1)}, u32[]{:S(2)}, u32[]{:S(2)}) async-start(f32[1,3,128,256]{3,0,1,2:T(1,128)} %copy.16), calls=%async_computation | async-start | bytes 786432 | tf_op jit(solution)/shard_map/all_to_all | solution.py:39
where the time goes:
time: 35.7 us; the launch traced here: 35.3 us
  waiting for transfers between devices  13.4 us (38%)
  starting transfers between devices  11 us (31%)
  other arithmetic  7.24 us (20%)
  local copies, waits for them, and re-layouts  2.94 us (8%)
  between operations  0.8 us (2%)
    all_to_all x1, waiting for transfers between devices, on_device(): lax.all_to_all(radiance[None], 'depth', split_axis=2, concat_axis=0, tile...  10.5 us
    all_to_all x1, starting transfers between devices, on_device(): lax.all_to_all(transmit[None, None], 'depth', split_axis=2, concat_axis=0...  7.41 us
    all_to_all x1, starting transfers between devices, on_device(): lax.all_to_all(radiance[None], 'depth', split_axis=2, concat_axis=0, tile...  3.55 us
    all_to_all x1, waiting for transfers between devices, on_device(): lax.all_to_all(transmit[None, None], 'depth', split_axis=2, concat_axis=0...  2.87 us
    mul x1, other arithmetic, march(): weight = (1.0 - jnp.exp(-optical)) * jnp.exp(-ahead)  2.56 us
    another operation x1, other arithmetic, march(): column = jnp.cumsum(optical, axis=0)  1.8 us
    another operation x1, other arithmetic, composite(): backward = jnp.flip(jnp.cumprod(jnp.flip(transmit, 0), axis=0), 0)  1.37 us
    broadcast_in_dim x1, local copies, waits for them, and re-layouts, on_device(): radiance[None]  1.14 us
  transfers between devices with their start and end apart: 2, of which 2 were waited for; matrix products, arithmetic and copies ran while one was open for 17% of the time, Pallas kernels for 0%

commit v1 on v0

v1 whole, which is shorter than its diff:
```python
import functools
import math

import jax
import jax.numpy as jnp
from jax import lax
from jax.experimental import pallas as pl
from jax.experimental.pallas import tpu as pltpu
from jax.sharding import PartitionSpec as P

ROWS = 8


def march_body(sel, facing, occupied, dense, emitted, out, dense_buf, emitted_buf, dense_sem, emitted_sem, *, chunks, tile_rows, bricks):
    depth_len, pairs, _, rows, width = dense.shape
    tiles_h, tiles_w = occupied.shape
    per = pairs // chunks
    half = sel[0]
    backward = facing[0] != 0

    def copies(chunk):
        span = pl.ds(chunk * per, per)
        return (
            pltpu.make_async_copy(dense.at[:, span, half], dense_buf.at[:, span], dense_sem.at[chunk]),
            pltpu.make_async_copy(emitted.at[:, :, span, half], emitted_buf.at[:, :, span], emitted_sem.at[chunk]),
        )

    for chunk in range(chunks):
        for copy in copies(chunk):
            copy.start()

    lane = lax.broadcasted_iota(jnp.int32, (ROWS, width), 1) // (width // tiles_w)
    scale = -math.log2(math.e) / (depth_len * bricks)

    for chunk in range(chunks):
        for copy in copies(chunk):
            copy.wait()

        def group(index, _, chunk=chunk):
            pair = chunk * per + index // (rows // ROWS)
            sub = index % (rows // ROWS)
            first = (pair * 2 + half) * rows + sub * ROWS
            tile = first // tile_rows
            gate = jnp.zeros((ROWS, width), jnp.float32)
            for column in range(tiles_w):
                gate = jnp.where(lane == column, occupied[tile, column].astype(jnp.float32) * scale, gate)
            span = pl.ds(pl.multiple_of(sub * ROWS, ROWS), ROWS)
            total = jnp.zeros((ROWS, width), jnp.float32)
            before = jnp.ones((ROWS, width), jnp.float32)
            colour = [jnp.zeros((ROWS, width), jnp.float32) for _ in range(3)]
            for step in range(depth_len):
                cell = jnp.where(backward, depth_len - 1 - step, step)
                total = total + dense_buf[cell, pair, span, :]
                after = jnp.exp2(total * gate)
                weight = before - after
                before = after
                for channel in range(3):
                    colour[channel] = colour[channel] + emitted_buf[channel, cell, pair, span, :].astype(jnp.float32) * weight
            for channel in range(3):
                out[pair, sub, channel] = colour[channel]
            out[pair, sub, 3] = before
            return 0

        lax.fori_loop(0, per * (rows // ROWS), group, 0)


def march(dense, emitted, occupied, facing, half, bricks):
    depth_len, pairs, _, rows, width = dense.shape
    tile_rows = pairs * 2 * rows // occupied.shape[0]
    chunks = math.gcd(pairs, 4)
    smem = pl.BlockSpec(memory_space=pltpu.SMEM)
    hbm = pl.BlockSpec(memory_space=pl.ANY)
    return pl.pallas_call(
        functools.partial(march_body, chunks=chunks, tile_rows=tile_rows, bricks=bricks),
        in_specs=[smem, smem, smem, hbm, hbm],
        out_specs=pl.BlockSpec(memory_space=pltpu.VMEM),
        out_shape=jax.ShapeDtypeStruct((pairs, rows // ROWS, 4, ROWS, width), jnp.float32),
        scratch_shapes=[
            pltpu.VMEM((depth_len, pairs, rows, width), jnp.float32),
            pltpu.VMEM((3, depth_len, pairs, rows, width), jnp.bfloat16),
            pltpu.SemaphoreType.DMA((chunks,)),
            pltpu.SemaphoreType.DMA((chunks,)),
        ],
        name="march",
    )(half, facing, occupied, dense, emitted)


def over(mine, other, nearer):
    colour, through = mine[..., :3, :, :], mine[..., 3:, :, :]
    colour_other, through_other = other[..., :3, :, :], other[..., 3:, :, :]
    merged = jnp.where(nearer, colour + through * colour_other, colour_other + through_other * colour)
    return jnp.concatenate([merged, through * through_other], axis=-3)


def swap(value, bit, size):
    return lax.ppermute(value, "depth", [(i, i ^ bit) for i in range(size)])


def halves(value, bit, place, axis):
    own = (place // bit) % 2
    keep = lax.dynamic_index_in_dim(value, own, axis, keepdims=False)
    give = lax.dynamic_index_in_dim(value, 1 - own, axis, keepdims=False)
    return keep, give


def on_device(density, emission, occupancy, facing):
    size = lax.axis_size("depth")
    place = lax.axis_index("depth")
    forward = facing[0] == 0
    depth_len, height, width = density.shape
    rows = height // size

    def nearer(bit):
        return ((place // bit) % 2 == 0) == forward

    own = (place % 2).astype(jnp.int32)
    if rows % ROWS == 0:
        pairs, unit = size // 2, rows
    else:
        pairs, unit = height // (2 * ROWS), ROWS
    dense = density.reshape(depth_len, pairs, 2, unit, width)
    emitted = emission.reshape(3, depth_len, pairs, 2, unit, width)
    if rows % ROWS == 0:
        give = march(dense, emitted, occupancy[0], facing, (1 - own)[None], size)
        got = swap(give, 1, size)
        keep = march(dense, emitted, occupancy[0], facing, own[None], size)
    else:
        both = jnp.stack([march(dense, emitted, occupancy[0], facing, jnp.full((1,), k, jnp.int32), size) for k in range(2)], axis=1)
        both = jnp.moveaxis(both[:, :, 0], 2, 0).reshape(4, size // 2, 2, 1, rows, width)
        both = jnp.moveaxis(both, 0, 3)
        keep, give = halves(both, 1, place, 1)
        got = swap(give, 1, size)
    value = over(keep, got, nearer(1))

    bit = 2
    while bit < size:
        tiles = value.shape[0]
        if bit == 2 and tiles >= 4:
            value = value.reshape((tiles // 4, 2, 2) + value.shape[1:])
            mine, theirs = halves(value, 2 * bit, place, 1)
            keep, give_low = halves(mine, bit, place, 1)
            give_high, give_both = halves(theirs, bit, place, 1)
            got_both = swap(give_both, 3 * bit, size)
            got_high = swap(give_high, 2 * bit, size)
            got_low = swap(give_low, bit, size)
            value = over(over(keep, got_low, nearer(bit)), over(got_high, got_both, nearer(bit)), nearer(2 * bit))
            bit *= 4
        else:
            value = value.reshape((tiles // 2, 2) + value.shape[1:])
            keep, give = halves(value, bit, place, 1)
            value = over(keep, swap(give, bit, size), nearer(bit))
            bit *= 2
    value = jnp.moveaxis(value[0], 1, 0).reshape(4, rows, width)
    return jnp.concatenate([value[:3], 1.0 - value[3:]], axis=0)


def solution(mesh):
    return jax.shard_map(
        on_device,
        mesh=mesh,
        in_specs=(
            P(("views", "depth"), None, None),
            P("views", "depth", None, None),
            P(("views", "depth"), None, None),
            P("views"),
        ),
        out_specs=P("views", "depth", None),
        check_vma=False,
    )
```

time: 35.7 us -> 25 us (0.70)
  Pallas kernels: 0 us -> 6.64 us
  waiting for transfers between devices: 13.4 us -> 7.25 us
  other arithmetic: 7.24 us -> 2.55 us
  starting transfers between devices: 11 us -> 7.46 us
  local copies, waits for them, and re-layouts: 2.94 us -> 0.03 us
    all_to_all x2 -> x0, waiting for transfers between devices: 13.4 us -> none  [the longest x1 10.5 us: on_device(): lax.all_to_all(radiance[None], 'depth', split_axis=2, concat_axis=0, tile...]
    all_to_all x2 -> x0, starting transfers between devices: 11 us -> none  [the longest x1 7.41 us: on_device(): lax.all_to_all(transmit[None, None], 'depth', split_axis=2, concat_axis=0...]
    ppermute x0 -> x5, starting transfers between devices: none -> 7.46 us  [swap(): return lax.ppermute(value, 'depth', [(i, i ^ bit) for i in range(size)])]
    ppermute x0 -> x5, waiting for transfers between devices: none -> 7.25 us  [swap(): return lax.ppermute(value, 'depth', [(i, i ^ bit) for i in range(size)])]
    pallas_call x0 -> x2, Pallas kernels: none -> 6.64 us  [march(): pl.pallas_call(functools.partial(march_body, chunks=chunks, tile_rows=til...]
    another operation x3 -> x0, other arithmetic: 3.24 us -> none  [the longest x1 1.8 us: march(): column = jnp.cumsum(optical, axis=0)]
    mul x2 -> x3, other arithmetic: 2.59 us -> 0.87 us  [the longest x2 0.86 us: over(): through * colour_other]
    broadcast_in_dim x1 -> x0, local copies, waits for them, and re-layouts: 1.14 us -> none  [on_device(): radiance[None]]
  transfers between devices with their start and end apart: 2 -> 5, of which waited for: 2 -> 4; matrix products, arithmetic and copies ran while one was open for 17% -> 0% of each run, Pallas kernels for 0% -> 13%
where the time goes in v1:
time: 25 us; the launch traced here: 24.7 us
  starting transfers between devices  7.46 us (30%)
  waiting for transfers between devices  7.25 us (29%)
  Pallas kernels  6.64 us (27%)
  other arithmetic  2.55 us (10%)
  between operations  0.77 us (3%)
    ppermute x5, starting transfers between devices, swap(): return lax.ppermute(value, 'depth', [(i, i ^ bit) for i in range(size)])  7.46 us
    ppermute x5, waiting for transfers between devices, swap(): return lax.ppermute(value, 'depth', [(i, i ^ bit) for i in range(size)])  7.25 us
    pallas_call x2, Pallas kernels, march(): pl.pallas_call(functools.partial(march_body, chunks=chunks, tile_rows=til...  6.64 us
    select_n x2, other arithmetic, over(): jnp.where(nearer, colour + through * colour_other, colour_other + through...  1.02 us
    mul x2, other arithmetic, over(): through * colour_other  0.86 us
    concatenate x1, other arithmetic, on_device(): return jnp.concatenate([value[:3], 1.0 - value[3:]], axis=0)  0.62 us
  transfers between devices with their start and end apart: 5, of which 4 were waited for; matrix products, arithmetic and copies ran while one was open for 0% of the time, Pallas kernels for 13%

profile of v1, /device:TPU:0, one launch (start us, length us, event | category | flops | bytes accessed | tf_op | source)
XLA Modules:
  0.0 24.7 jit_solution(6548497613009579832)
XLA Ops:
  0.7 3.3 %march.3 = f32[8,1,4,8,256]{4,3,2,1,0:T(8,128)} custom-call(s32[1]{0:T(128)} %bitcast.6.sel, s32[1]{0:T(128)S(6)} %copy.5.facing, s32[4,4]{1,0:T(4,128)} %bitcast.44, f32[16,8,2,8,256]{4,3,2,1,0:T(8,128)} %bitcast.41, bf16[3,16,8,2,8,256]{5,4,3,2,1,0:T(8,128)(2,1)} %bitcast.39), custom_call_target="tpu_custom_call" | custom-call | tf_op jit(solution)/shard_map/march/pallas_call | solution.py:73
  4.0 0.6 %collective-permute-start = (f32[8,1,4,8,256]{4,3,2,1,0:T(8,128)}, f32[8,1,4,8,256]{4,3,2,1,0:T(8,128)S(1)}, u32[]{:S(2)}, u32[]{:S(2)}) collective-permute-start(f32[8,1,4,8,256]{4,3,2,1,0:T(8,128)} %march.3), channel_id=1, source_target_pairs={{0,1},{1,0},{2,3},{3,2},{4,5},{5,4},{6,7},{7,6},{8,9},{9,8},{10,11... | collective-permute-start | bytes 786440 | tf_op jit(solution)/shard_map/ppermute | solution.py:96
  4.5 3.3 %march.2 = f32[8,1,4,8,256]{4,3,2,1,0:T(8,128)} custom-call(s32[1]{0:T(128)} %bitcast.1.sel, s32[1]{0:T(128)S(6)} %copy.5.facing, s32[4,4]{1,0:T(4,128)} %bitcast.45, f32[16,8,2,8,256]{4,3,2,1,0:T(8,128)} %bitcast.42, bf16[3,16,8,2,8,256]{5,4,3,2,1,0:T(8,128)(2,1)} %bitcast.40), custom_call_target="tpu_custom_call" | custom-call | tf_op jit(solution)/shard_map/march/pallas_call | solution.py:73
  7.9 0.0 collective-permute-done
  7.9 0.9 %slice_bitcast_fusion.1 = (f32[8,8,256]{2,1,0:T(8,128)S(1)}, f32[8,1,1,8,256]{4,3,2,1,0:T(8,128)S(1)}, f32[8,8,256]{2,1,0:T(8,128)S(1)}) fusion(f32[8,1,4,8,256]{4,3,2,1,0:T(8,128)} %march.2, f32[8,1,4,8,256]{4,3,2,1,0:T(8,128)S(1)} %collective-permute-done), kind=kLoop, calls=%fused_computation.12 | loop fusion | flops 16384 | bytes 327680 | tf_op jit(solution)/shard_map/mul | solution.py:91
  8.8 1.0 %add_select_fusion = f32[8,1,3,8,256]{4,3,2,1,0:T(8,128)S(1)} fusion(f32[8,1,4,8,256]{4,3,2,1,0:T(8,128)} %march.2, f32[8,1,4,8,256]{4,3,2,1,0:T(8,128)S(1)} %collective-permute-done, f32[8,8,256]{2,1,0:T(8,128)S(1)} %get-tuple-element.11, f32[8,8,256]{2,1,0:T(8,128)S(1)} %get-tuple-element.9, pred[]{:T(512)S(6)} %eq.52), kind=kLoop, calls=%fused_computation.1 | loop fusion | flops 245760 | bytes 720897 | tf_op jit(solution)/shard_map/jit(_where)/select_n | solution.py:91
  9.8 2.7 %collective-permute-start.2 = (f32[2,1,4,8,256]{4,3,2,1,0:T(8,128)S(1)}, f32[2,1,4,8,256]{4,3,2,1,0:T(8,128)S(1)}, u32[]{:S(2)}, u32[]{:S(2)}) collective-permute-start(f32[2,1,4,8,256]{4,3,2,1,0:T(8,128)S(1)} %get-tuple-element.7), channel_id=1, source_target_pairs={{0,4},{1,5},{2,6},{3,7},{4,0},{5,1},{6,2},{7,3},{8,12},{9,13},{10,... | collective-permute-start | bytes 196616 | tf_op jit(solution)/shard_map/ppermute | solution.py:96
  12.5 1.4 %collective-permute-start.3 = (f32[2,1,4,8,256]{4,3,2,1,0:T(8,128)S(1)}, f32[2,1,4,8,256]{4,3,2,1,0:T(8,128)S(1)}, u32[]{:S(2)}, u32[]{:S(2)}) collective-permute-start(f32[2,1,4,8,256]{4,3,2,1,0:T(8,128)S(1)} %get-tuple-element.6), channel_id=1, source_target_pairs={{0,6},{1,7},{2,4},{3,5},{4,2},{5,3},{6,0},{7,1},{8,14},{9,15},{10,... | collective-permute-start | bytes 196616 | tf_op jit(solution)/shard_map/ppermute | solution.py:96
  14.0 0.1 collective-permute-start.1
  14.1 1.1 %collective-permute-done.2 = f32[2,1,4,8,256]{4,3,2,1,0:T(8,128)S(1)} collective-permute-done((f32[2,1,4,8,256]{4,3,2,1,0:T(8,128)S(1)}, f32[2,1,4,8,256]{4,3,2,1,0:T(8,128)S(1)}, u32[]{:S(2)}, u32[]{:S(2)}) %collective-permute-start.2) | collective-permute-done | bytes 65568 | tf_op jit(solution)/shard_map/ppermute | solution.py:96
  15.2 2.6 %collective-permute-done.3 = f32[2,1,4,8,256]{4,3,2,1,0:T(8,128)S(1)} collective-permute-done((f32[2,1,4,8,256]{4,3,2,1,0:T(8,128)S(1)}, f32[2,1,4,8,256]{4,3,2,1,0:T(8,128)S(1)}, u32[]{:S(2)}, u32[]{:S(2)}) %collective-permute-start.3) | collective-permute-done | bytes 65568 | tf_op jit(solution)/shard_map/ppermute | solution.py:96
  17.9 1.3 %collective-permute-done.1 = f32[2,1,4,8,256]{4,3,2,1,0:T(8,128)S(1)} collective-permute-done((f32[2,1,4,8,256]{4,3,2,1,0:T(8,128)S(1)}, f32[2,1,4,8,256]{4,3,2,1,0:T(8,128)S(1)}, u32[]{:S(2)}, u32[]{:S(2)}) %collective-permute-start.1) | collective-permute-done | bytes 65568 | tf_op jit(solution)/shard_map/ppermute | solution.py:96
  19.2 2.7 %collective-permute-start.4 = (f32[1,1,4,8,256]{4,3,2,1,0:T(8,128)S(1)}, f32[1,1,4,8,256]{4,3,2,1,0:T(8,128)S(1)}, u32[]{:S(2)}, u32[]{:S(2)}) collective-permute-start(f32[1,1,4,8,256]{4,3,2,1,0:T(8,128)S(1)} %get-tuple-element.16), channel_id=1, source_target_pairs={{0,8},{1,9},{2,10},{3,11},{4,12},{5,13},{6,14},{7,15},{8,0},{9,1},... | collective-permute-start | bytes 98312 | tf_op jit(solution)/shard_map/ppermute | solution.py:96
  21.8 2.2 %collective-permute-done.4 = f32[1,1,4,8,256]{4,3,2,1,0:T(8,128)S(1)} collective-permute-done((f32[1,1,4,8,256]{4,3,2,1,0:T(8,128)S(1)}, f32[1,1,4,8,256]{4,3,2,1,0:T(8,128)S(1)}, u32[]{:S(2)}, u32[]{:S(2)}) %collective-permute-start.4) | collective-permute-done | bytes 32800 | tf_op jit(solution)/shard_map/ppermute | solution.py:96
  24.1 0.6 %pad_maximum_fusion.1 = f32[4,8,256]{2,1,0:T(8,128)} fusion(f32[1,8,256]{2,1,0:T(8,128)S(1)} %get-tuple-element.22, f32[3,8,256]{2,1,0:T(8,128)S(1)} %select_bitcast_fusion), kind=kLoop, calls=%fused_computation.16 | loop fusion | flops 8192 | bytes 65536 | tf_op jit(solution)/shard_map/concatenate | solution.py:154
  (7 shorter events, 0.1 us)
Async XLA Ops:
  4.0 3.9 %collective-permute-start = (f32[8,1,4,8,256]{4,3,2,1,0:T(8,128)}, f32[8,1,4,8,256]{4,3,2,1,0:T(8,128)S(1)}, u32[]{:S(2)}, u32[]{:S(2)}) collective-permute-start(f32[8,1,4,8,256]{4,3,2,1,0:T(8,128)} %march.3), channel_id=1, source_target_pairs={{0,1},{1,0},{2,3},{3,2},{4,5},{5,4},{6,7},{7,6},{8,9},{9,8},{10,11... | collective-permute-start | bytes 786440 | tf_op jit(solution)/shard_map/ppermute | solution.py:96
  9.8 5.4 %collective-permute-start.2 = (f32[2,1,4,8,256]{4,3,2,1,0:T(8,128)S(1)}, f32[2,1,4,8,256]{4,3,2,1,0:T(8,128)S(1)}, u32[]{:S(2)}, u32[]{:S(2)}) collective-permute-start(f32[2,1,4,8,256]{4,3,2,1,0:T(8,128)S(1)} %get-tuple-element.7), channel_id=1, source_target_pairs={{0,4},{1,5},{2,6},{3,7},{4,0},{5,1},{6,2},{7,3},{8,12},{9,13},{10,... | collective-permute-start | bytes 196616 | tf_op jit(solution)/shard_map/ppermute | solution.py:96
  12.5 5.3 %collective-permute-start.3 = (f32[2,1,4,8,256]{4,3,2,1,0:T(8,128)S(1)}, f32[2,1,4,8,256]{4,3,2,1,0:T(8,128)S(1)}, u32[]{:S(2)}, u32[]{:S(2)}) collective-permute-start(f32[2,1,4,8,256]{4,3,2,1,0:T(8,128)S(1)} %get-tuple-element.6), channel_id=1, source_target_pairs={{0,6},{1,7},{2,4},{3,5},{4,2},{5,3},{6,0},{7,1},{8,14},{9,15},{10,... | collective-permute-start | bytes 196616 | tf_op jit(solution)/shard_map/ppermute | solution.py:96
  14.0 5.2 %collective-permute-start.1 = (f32[2,1,4,8,256]{4,3,2,1,0:T(8,128)S(1)}, f32[2,1,4,8,256]{4,3,2,1,0:T(8,128)S(1)}, u32[]{:S(2)}, u32[]{:S(2)}) collective-permute-start(f32[2,1,4,8,256]{4,3,2,1,0:T(8,128)S(1)} %get-tuple-element.5), channel_id=1, source_target_pairs={{0,2},{1,3},{2,0},{3,1},{4,6},{5,7},{6,4},{7,5},{8,10},{9,11},{10,... | collective-permute-start | bytes 196616 | tf_op jit(solution)/shard_map/ppermute | solution.py:96
  19.2 4.9 %collective-permute-start.4 = (f32[1,1,4,8,256]{4,3,2,1,0:T(8,128)S(1)}, f32[1,1,4,8,256]{4,3,2,1,0:T(8,128)S(1)}, u32[]{:S(2)}, u32[]{:S(2)}) collective-permute-start(f32[1,1,4,8,256]{4,3,2,1,0:T(8,128)S(1)} %get-tuple-element.16), channel_id=1, source_target_pairs={{0,8},{1,9},{2,10},{3,11},{4,12},{5,13},{6,14},{7,15},{8,0},{9,1},... | collective-permute-start | bytes 98312 | tf_op jit(solution)/shard_map/ppermute | solution.py:96

commit v2 on v1

v2 whole, which is shorter than its diff:
```python
import functools
import math

import jax
import jax.numpy as jnp
from jax import lax
from jax.experimental import pallas as pl
from jax.experimental.pallas import tpu as pltpu
from jax.sharding import PartitionSpec as P

ROWS = 8
CROSSING = ~4


def parity(chip_bits):
    for shift in (8, 4, 2, 1):
        chip_bits = chip_bits ^ (chip_bits >> shift)
    return chip_bits & 1


def side(pair):
    return parity((pair * 2) & CROSSING & 0xFFFE)


def march_body(facing, occupied_hbm, dense, emitted, out, dense_buf, emitted_buf, occupied, dense_sem, emitted_sem, small_sem, *, other, tile_rows, bricks):
    depth_len, pairs, _, rows, width = dense.shape
    tiles_h, tiles_w = occupied.shape
    place = lax.axis_index("depth")
    chosen = ((place & 1) ^ side(place >> 1)) ^ int(other)

    small = pltpu.make_async_copy(occupied_hbm, occupied, small_sem)
    small.start()

    def copies(pair):
        half = chosen ^ side(pair)
        return (
            pltpu.make_async_copy(dense.at[:, pair, half], dense_buf.at[:, pair], dense_sem.at[pair]),
            pltpu.make_async_copy(emitted.at[:, :, pair, half], emitted_buf.at[:, :, pair], emitted_sem.at[pair]),
        )

    for pair in range(pairs):
        for copy in copies(pair):
            copy.start()

    lane = lax.broadcasted_iota(jnp.int32, (ROWS, width), 1) // (width // tiles_w)
    scale = -math.log2(math.e) / (depth_len * bricks)
    small.wait()
    backward = facing[0] != 0

    def march_pair(pair, _):
        for copy in copies(pair):
            copy.wait()
        half = chosen ^ side(pair)
        for sub in range(rows // ROWS):
            tile = ((pair * 2 + half) * rows + sub * ROWS) // tile_rows
            gate = jnp.zeros((ROWS, width), jnp.float32)
            for column in range(tiles_w):
                gate = jnp.where(lane == column, occupied[tile, column].astype(jnp.float32) * scale, gate)
            span = pl.ds(sub * ROWS, ROWS)
            total = jnp.zeros((ROWS, width), jnp.float32)
            before = jnp.ones((ROWS, width), jnp.float32)
            colour = [jnp.zeros((ROWS, width), jnp.float32) for _ in range(3)]
            for step in range(depth_len):
                cell = jnp.where(backward, depth_len - 1 - step, step)
                total = total + dense_buf[cell, pair, span, :]
                after = jnp.exp2(total * gate)
                weight = before - after
                before = after
                for channel in range(3):
                    colour[channel] = colour[channel] + emitted_buf[channel, cell, pair, span, :].astype(jnp.float32) * weight
            for channel in range(3):
                out[pair, sub, channel] = colour[channel]
            out[pair, sub, 3] = before
        return 0

    lax.fori_loop(0, pairs, march_pair, 0)


def march(dense, emitted, occupied, facing, other, bricks):
    depth_len, pairs, _, rows, width = dense.shape
    tile_rows = pairs * 2 * rows // occupied.shape[0]
    hbm = pl.BlockSpec(memory_space=pl.ANY)
    return pl.pallas_call(
        functools.partial(march_body, other=other, tile_rows=tile_rows, bricks=bricks),
        in_specs=[pl.BlockSpec(memory_space=pltpu.SMEM), hbm, hbm, hbm],
        out_specs=pl.BlockSpec(memory_space=pltpu.VMEM),
        out_shape=pltpu.VMEM((pairs, rows // ROWS, 4, ROWS, width), jnp.float32),
        scratch_shapes=[
            pltpu.VMEM((depth_len, pairs, rows, width), jnp.float32),
            pltpu.VMEM((3, depth_len, pairs, rows, width), jnp.bfloat16),
            pltpu.SMEM(occupied.shape, jnp.int32),
            pltpu.SemaphoreType.DMA((pairs,)),
            pltpu.SemaphoreType.DMA((pairs,)),
            pltpu.SemaphoreType.DMA,
        ],
        name="march",
    )(facing, occupied, dense, emitted)


def over(mine, other, nearer):
    colour, through = mine[..., :3, :, :], mine[..., 3:, :, :]
    colour_other, through_other = other[..., :3, :, :], other[..., 3:, :, :]
    merged = jnp.where(nearer, colour + through * colour_other, colour_other + through_other * colour)
    return jnp.concatenate([merged, through * through_other], axis=-3)


def swap(value, mask, size):
    mask = mask | parity(mask & CROSSING & 0xFFFE)
    return lax.ppermute(value, "depth", [(i, i ^ mask) for i in range(size)])


def halves(value, bit, place):
    own = jnp.minimum(place & bit, 1)
    keep = lax.dynamic_index_in_dim(value, own, 1, keepdims=False)
    give = lax.dynamic_index_in_dim(value, 1 - own, 1, keepdims=False)
    return keep, give


def on_device(density, emission, occupancy, facing):
    size = lax.axis_size("depth")
    place = lax.axis_index("depth")
    depth_len, height, width = density.shape
    rows = height // size
    aligned = rows % ROWS == 0
    pairs, unit = (size // 2, rows) if aligned else (height // (2 * ROWS), ROWS)
    dense = density.reshape(depth_len, pairs, 2, unit, width)
    emitted = emission.reshape(3, depth_len, pairs, 2, unit, width)

    give = march(dense, emitted, occupancy[0], facing, True, size)
    keep = march(dense, emitted, occupancy[0], facing, False, size)
    if not aligned:
        pair = jnp.arange(pairs)
        chosen = ((place & 1) ^ side(place >> 1)) ^ side(pair)
        swapped = (chosen == 1)[:, None, None, None]
        both = jnp.stack([jnp.where(swapped, give[:, 0], keep[:, 0]), jnp.where(swapped, keep[:, 0], give[:, 0])], axis=1)
        both = jnp.moveaxis(both, 2, 0).reshape(4, size // 2, 2, 1, rows, width)
        both = jnp.moveaxis(both, 0, 3)
        pair = jnp.arange(size // 2)
        swapped = ((((place & 1) ^ side(place >> 1)) ^ side(pair)) == 1)[:, None, None, None, None]
        keep = jnp.where(swapped, both[:, 1], both[:, 0])
        give = jnp.where(swapped, both[:, 0], both[:, 1])
    forward = facing[0] == 0

    def nearer(bit):
        return ((place & bit) == 0) == forward

    value = over(keep, swap(give, 1, size), nearer(1))
    bit = 2
    while bit < size:
        tiles = value.shape[0]
        if bit == 2 and tiles >= 4:
            value = value.reshape((tiles // 4, 2, 2) + value.shape[1:])
            mine, theirs = halves(value, 2 * bit, place)
            keep, give_low = halves(mine, bit, place)
            give_high, give_both = halves(theirs, bit, place)
            got_both = swap(give_both, 3 * bit, size)
            got_high = swap(give_high, 2 * bit, size)
            got_low = swap(give_low, bit, size)
            value = over(over(keep, got_low, nearer(bit)), over(got_high, got_both, nearer(bit)), nearer(2 * bit))
            bit *= 4
        else:
            value = value.reshape((tiles // 2, 2) + value.shape[1:])
            keep, give = halves(value, bit, place)
            value = over(keep, swap(give, bit, size), nearer(bit))
            bit *= 2
    value = jnp.moveaxis(value[0], 1, 0).reshape(4, rows, width)
    return jnp.concatenate([value[:3], 1.0 - value[3:]], axis=0)


def solution(mesh):
    return jax.shard_map(
        on_device,
        mesh=mesh,
        in_specs=(
            P(("views", "depth"), None, None),
            P("views", "depth", None, None),
            P(("views", "depth"), None, None),
            P("views"),
        ),
        out_specs=P("views", "depth", None),
        check_vma=False,
    )
```

time: 25 us -> 21.1 us (0.84)
  Pallas kernels: 6.64 us -> 4.08 us
  other arithmetic: 2.55 us -> 0.78 us
  waiting for transfers between devices: 7.25 us -> 8.14 us
  starting transfers between devices: 7.46 us -> 7.12 us
    pallas_call x2, Pallas kernels: 6.64 us -> 4.08 us  [march(): pl.pallas_call(functools.partial(march_body, other=other, tile_rows=tile_...]
    select_n x2, other arithmetic: 1.02 us -> 0.09 us  [over(): jnp.where(nearer, colour + through * colour_other, colour_other + through...]
    ppermute x5, waiting for transfers between devices: 7.25 us -> 8.14 us  [swap(): return lax.ppermute(value, 'depth', [(i, i ^ mask) for i in range(size)])]
    mul x2, other arithmetic: 0.86 us -> 0.02 us  [over(): through * colour_other]
    ppermute x5, starting transfers between devices: 7.46 us -> 7.12 us  [swap(): return lax.ppermute(value, 'depth', [(i, i ^ mask) for i in range(size)])]
  transfers between devices with their start and end apart: 5 -> 5, of which waited for: 4 -> 4; matrix products, arithmetic and copies ran while one was open for 0% -> 0% of each run, Pallas kernels for 13% -> 10%
where the time goes in v2:
time: 21.1 us; the launch traced here: 20.9 us
  waiting for transfers between devices  8.14 us (39%)
  starting transfers between devices  7.12 us (34%)
  Pallas kernels  4.08 us (19%)
  other arithmetic  0.78 us (4%)
  between operations  0.76 us (4%)
    ppermute x5, waiting for transfers between devices, swap(): return lax.ppermute(value, 'depth', [(i, i ^ mask) for i in range(size)])  8.14 us
    ppermute x5, starting transfers between devices, swap(): return lax.ppermute(value, 'depth', [(i, i ^ mask) for i in range(size)])  7.12 us
    pallas_call x2, Pallas kernels, march(): pl.pallas_call(functools.partial(march_body, other=other, tile_rows=tile_...  4.08 us
    concatenate x1, other arithmetic, on_device(): return jnp.concatenate([value[:3], 1.0 - value[3:]], axis=0)  0.62 us
  transfers between devices with their start and end apart: 5, of which 4 were waited for; matrix products, arithmetic and copies ran while one was open for 0% of the time, Pallas kernels for 10%

profile of v2, /device:TPU:0, one launch (start us, length us, event | category | flops | bytes accessed | tf_op | source)
XLA Modules:
  0.0 20.9 jit_solution(10143118462191354430)
XLA Ops:
  0.7 2.0 %march.3 = f32[8,1,4,8,256]{4,3,2,1,0:T(8,128)S(1)} custom-call(s32[1]{0:T(128)S(6)} %copy.5.facing, s32[4,4]{1,0:T(4,128)} %bitcast.42, f32[16,8,2,8,256]{4,3,2,1,0:T(8,128)} %bitcast.39, bf16[3,16,8,2,8,256]{5,4,3,2,1,0:T(8,128)(2,1)} %bitcast.37), custom_call_target="tpu_custom_call" | custom-call | tf_op jit(solution)/shard_map/march/pallas_call | solution.py:83
  2.7 0.6 %collective-permute-start = (f32[8,1,4,8,256]{4,3,2,1,0:T(8,128)S(1)}, f32[8,1,4,8,256]{4,3,2,1,0:T(8,128)S(1)}, u32[]{:S(2)}, u32[]{:S(2)}) collective-permute-start(f32[8,1,4,8,256]{4,3,2,1,0:T(8,128)S(1)} %march.3), channel_id=1, source_target_pairs={{0,1},{1,0},{2,3},{3,2},{4,5},{5,4},{6,7},{7,6},{8,9},{9,8},{10,11... | collective-permute-start | bytes 786440 | tf_op jit(solution)/shard_map/ppermute | solution.py:109
  3.3 2.0 %march.2 = f32[8,1,4,8,256]{4,3,2,1,0:T(8,128)S(1)} custom-call(s32[1]{0:T(128)S(6)} %copy.5.facing, s32[4,4]{1,0:T(4,128)} %bitcast.43, f32[16,8,2,8,256]{4,3,2,1,0:T(8,128)} %bitcast.40, bf16[3,16,8,2,8,256]{5,4,3,2,1,0:T(8,128)(2,1)} %bitcast.38), custom_call_target="tpu_custom_call" | custom-call | tf_op jit(solution)/shard_map/march/pallas_call | solution.py:83
  5.3 0.0 collective-permute-done
  5.5 2.7 %collective-permute-start.1 = (f32[2,1,4,8,256]{4,3,2,1,0:T(8,128)S(1)}, f32[2,1,4,8,256]{4,3,2,1,0:T(8,128)S(1)}, u32[]{:S(2)}, u32[]{:S(2)}) collective-permute-start(f32[2,1,4,8,256]{4,3,2,1,0:T(8,128)S(1)} %get-tuple-element.5), channel_id=1, source_target_pairs={{0,3},{1,2},{2,1},{3,0},{4,7},{5,6},{6,5},{7,4},{8,11},{9,10},{10,... | collective-permute-start | bytes 196616 | tf_op jit(solution)/shard_map/ppermute | solution.py:109
  8.2 1.6 %collective-permute-start.2 = (f32[2,1,4,8,256]{4,3,2,1,0:T(8,128)S(1)}, f32[2,1,4,8,256]{4,3,2,1,0:T(8,128)S(1)}, u32[]{:S(2)}, u32[]{:S(2)}) collective-permute-start(f32[2,1,4,8,256]{4,3,2,1,0:T(8,128)S(1)} %get-tuple-element.7), channel_id=1, source_target_pairs={{0,4},{1,5},{2,6},{3,7},{4,0},{5,1},{6,2},{7,3},{8,12},{9,13},{10,... | collective-permute-start | bytes 196616 | tf_op jit(solution)/shard_map/ppermute | solution.py:109
  9.8 0.0 collective-permute-start.3
  9.8 0.9 %collective-permute-done.1 = f32[2,1,4,8,256]{4,3,2,1,0:T(8,128)S(1)} collective-permute-done((f32[2,1,4,8,256]{4,3,2,1,0:T(8,128)S(1)}, f32[2,1,4,8,256]{4,3,2,1,0:T(8,128)S(1)}, u32[]{:S(2)}, u32[]{:S(2)}) %collective-permute-start.1) | collective-permute-done | bytes 65568 | tf_op jit(solution)/shard_map/ppermute | solution.py:109
  10.6 1.8 %collective-permute-done.2 = f32[2,1,4,8,256]{4,3,2,1,0:T(8,128)S(1)} collective-permute-done((f32[2,1,4,8,256]{4,3,2,1,0:T(8,128)S(1)}, f32[2,1,4,8,256]{4,3,2,1,0:T(8,128)S(1)}, u32[]{:S(2)}, u32[]{:S(2)}) %collective-permute-start.2) | collective-permute-done | bytes 65568 | tf_op jit(solution)/shard_map/ppermute | solution.py:109
  12.4 2.5 %collective-permute-done.3 = f32[2,1,4,8,256]{4,3,2,1,0:T(8,128)S(1)} collective-permute-done((f32[2,1,4,8,256]{4,3,2,1,0:T(8,128)S(1)}, f32[2,1,4,8,256]{4,3,2,1,0:T(8,128)S(1)}, u32[]{:S(2)}, u32[]{:S(2)}) %collective-permute-start.3) | collective-permute-done | bytes 65568 | tf_op jit(solution)/shard_map/ppermute | solution.py:109
  15.1 2.3 %collective-permute-start.4 = (f32[1,1,4,8,256]{4,3,2,1,0:T(8,128)S(1)}, f32[1,1,4,8,256]{4,3,2,1,0:T(8,128)S(1)}, u32[]{:S(2)}, u32[]{:S(2)}) collective-permute-start(f32[1,1,4,8,256]{4,3,2,1,0:T(8,128)S(1)} %get-tuple-element.16), channel_id=1, source_target_pairs={{0,9},{1,8},{2,11},{3,10},{4,13},{5,12},{6,15},{7,14},{8,1},{9,0},... | collective-permute-start | bytes 98312 | tf_op jit(solution)/shard_map/ppermute | solution.py:109
  17.4 2.9 %collective-permute-done.4 = f32[1,1,4,8,256]{4,3,2,1,0:T(8,128)S(1)} collective-permute-done((f32[1,1,4,8,256]{4,3,2,1,0:T(8,128)S(1)}, f32[1,1,4,8,256]{4,3,2,1,0:T(8,128)S(1)}, u32[]{:S(2)}, u32[]{:S(2)}) %collective-permute-start.4) | collective-permute-done | bytes 32800 | tf_op jit(solution)/shard_map/ppermute | solution.py:109
  20.3 0.6 %pad_maximum_fusion.1 = f32[4,8,256]{2,1,0:T(8,128)} fusion(f32[1,8,256]{2,1,0:T(8,128)S(1)} %get-tuple-element.22, f32[3,8,256]{2,1,0:T(8,128)S(1)} %select_bitcast_fusion), kind=kLoop, calls=%fused_computation.16 | loop fusion | flops 8192 | bytes 65536 | tf_op jit(solution)/shard_map/concatenate | solution.py:167
  (9 shorter events, 0.2 us)
Async XLA Ops:
  2.7 2.6 %collective-permute-start = (f32[8,1,4,8,256]{4,3,2,1,0:T(8,128)S(1)}, f32[8,1,4,8,256]{4,3,2,1,0:T(8,128)S(1)}, u32[]{:S(2)}, u32[]{:S(2)}) collective-permute-start(f32[8,1,4,8,256]{4,3,2,1,0:T(8,128)S(1)} %march.3), channel_id=1, source_target_pairs={{0,1},{1,0},{2,3},{3,2},{4,5},{5,4},{6,7},{7,6},{8,9},{9,8},{10,11... | collective-permute-start | bytes 786440 | tf_op jit(solution)/shard_map/ppermute | solution.py:109
  5.5 5.1 %collective-permute-start.1 = (f32[2,1,4,8,256]{4,3,2,1,0:T(8,128)S(1)}, f32[2,1,4,8,256]{4,3,2,1,0:T(8,128)S(1)}, u32[]{:S(2)}, u32[]{:S(2)}) collective-permute-start(f32[2,1,4,8,256]{4,3,2,1,0:T(8,128)S(1)} %get-tuple-element.5), channel_id=1, source_target_pairs={{0,3},{1,2},{2,1},{3,0},{4,7},{5,6},{6,5},{7,4},{8,11},{9,10},{10,... | collective-permute-start | bytes 196616 | tf_op jit(solution)/shard_map/ppermute | solution.py:109
  8.2 4.3 %collective-permute-start.2 = (f32[2,1,4,8,256]{4,3,2,1,0:T(8,128)S(1)}, f32[2,1,4,8,256]{4,3,2,1,0:T(8,128)S(1)}, u32[]{:S(2)}, u32[]{:S(2)}) collective-permute-start(f32[2,1,4,8,256]{4,3,2,1,0:T(8,128)S(1)} %get-tuple-element.7), channel_id=1, source_target_pairs={{0,4},{1,5},{2,6},{3,7},{4,0},{5,1},{6,2},{7,3},{8,12},{9,13},{10,... | collective-permute-start | bytes 196616 | tf_op jit(solution)/shard_map/ppermute | solution.py:109
  9.8 5.2 %collective-permute-start.3 = (f32[2,1,4,8,256]{4,3,2,1,0:T(8,128)S(1)}, f32[2,1,4,8,256]{4,3,2,1,0:T(8,128)S(1)}, u32[]{:S(2)}, u32[]{:S(2)}) collective-permute-start(f32[2,1,4,8,256]{4,3,2,1,0:T(8,128)S(1)} %get-tuple-element.6), channel_id=1, source_target_pairs={{0,7},{1,6},{2,5},{3,4},{4,3},{5,2},{6,1},{7,0},{8,15},{9,14},{10,... | collective-permute-start | bytes 196616 | tf_op jit(solution)/shard_map/ppermute | solution.py:109
  15.1 5.2 %collective-permute-start.4 = (f32[1,1,4,8,256]{4,3,2,1,0:T(8,128)S(1)}, f32[1,1,4,8,256]{4,3,2,1,0:T(8,128)S(1)}, u32[]{:S(2)}, u32[]{:S(2)}) collective-permute-start(f32[1,1,4,8,256]{4,3,2,1,0:T(8,128)S(1)} %get-tuple-element.16), channel_id=1, source_target_pairs={{0,9},{1,8},{2,11},{3,10},{4,13},{5,12},{6,15},{7,14},{8,1},{9,0},... | collective-permute-start | bytes 98312 | tf_op jit(solution)/shard_map/ppermute | solution.py:109

commit v3 on v2

--- a/solution.py
+++ b/solution.py
@@ -8,7 +8,9 @@
 from jax.experimental.pallas import tpu as pltpu
 from jax.sharding import PartitionSpec as P
 
+
 ROWS = 8
+CHUNKS = 8
 CROSSING = ~4
 
 
@@ -22,24 +24,25 @@
     return parity((pair * 2) & CROSSING & 0xFFFE)
 
 
-def march_body(facing, occupied_hbm, dense, emitted, out, dense_buf, emitted_buf, occupied, dense_sem, emitted_sem, small_sem, *, other, tile_rows, bricks):
+def march_body(facing, occupied_hbm, dense, emitted, keep, give, dense_buf, emitted_buf, occupied, dense_sem, emitted_sem, small_sem, *, chunks, tile_rows, bricks):
     depth_len, pairs, _, rows, width = dense.shape
-    tiles_h, tiles_w = occupied.shape
+    _, tiles_w = occupied.shape
+    per = pairs // chunks
     place = lax.axis_index("depth")
-    chosen = ((place & 1) ^ side(place >> 1)) ^ int(other)
+    chosen = (place & 1) ^ side(place >> 1)
 
     small = pltpu.make_async_copy(occupied_hbm, occupied, small_sem)
     small.start()
 
-    def copies(pair):
-        half = chosen ^ side(pair)
+    def copies(chunk):
+        span = pl.ds(chunk * per, per)
         return (
-            pltpu.make_async_copy(dense.at[:, pair, half], dense_buf.at[:, pair], dense_sem.at[pair]),
-            pltpu.make_async_copy(emitted.at[:, :, pair, half], emitted_buf.at[:, :, pair], emitted_sem.at[pair]),
+            pltpu.make_async_copy(dense.at[:, span], dense_buf.at[:, span], dense_sem.at[chunk]),
+            pltpu.make_async_copy(emitted.at[:, :, span], emitted_buf.at[:, :, span], emitted_sem.at[chunk]),
         )
 
-    for pair in range(pairs):
-        for copy in copies(pair):
+    for chunk in range(chunks):
+        for copy in copies(chunk):
             copy.start()
 
     lane = lax.broadcasted_iota(jnp.int32, (ROWS, width), 1) // (width // tiles_w)
@@ -47,50 +50,59 @@
     small.wait()
     backward = facing[0] != 0
 
-    def march_pair(pair, _):
-        for copy in copies(pair):
+    def march_chunk(chunk, _):
+        for copy in copies(chunk):
             copy.wait()
-        half = chosen ^ side(pair)
-        for sub in range(rows // ROWS):
-            tile = ((pair * 2 + half) * rows + sub * ROWS) // tile_rows
-            gate = jnp.zeros((ROWS, width), jnp.float32)
-            for column in range(tiles_w):
-                gate = jnp.where(lane == column, occupied[tile, column].astype(jnp.float32) * scale, gate)
-            span = pl.ds(sub * ROWS, ROWS)
-            total = jnp.zeros((ROWS, width), jnp.float32)
-            before = jnp.ones((ROWS, width), jnp.float32)
-            colour = [jnp.zeros((ROWS, width), jnp.float32) for _ in range(3)]
-            for step in range(depth_len):
-                cell = jnp.where(backward, depth_len - 1 - step, step)
-                total = total + dense_buf[cell, pair, span, :]
-                after = jnp.exp2(total * gate)
-                weight = before - after
-                before = after
-                for channel in range(3):
-                    colour[channel] = colour[channel] + emitted_buf[channel, cell, pair, span, :].astype(jnp.float32) * weight
-            for channel in range(3):
-                out[pair, sub, channel] = colour[channel]
-            out[pair, sub, 3] = before
+
+        def march_pair(index, _):
+            pair = chunk * per + index
+            for other, out in ((0, keep), (1, give)):
+                half = chosen ^ side(pair) ^ other
+                for sub in range(rows // ROWS):
+                    tile = ((pair * 2 + half) * rows + sub * ROWS) // tile_rows
+                    gate = jnp.zeros((ROWS, width), jnp.float32)
+                    for column in range(tiles_w):
+                        gate = jnp.where(lane == column, occupied[tile, column].astype(jnp.float32) * scale, gate)
+                    span = pl.ds(sub * ROWS, ROWS)
+                    total = jnp.zeros((ROWS, width), jnp.float32)
+                    before = jnp.ones((ROWS, width), jnp.float32)
+                    colour = [jnp.zeros((ROWS, width), jnp.float32) for _ in range(3)]
+                    for step in range(depth_len):
+                        cell = jnp.where(backward, depth_len - 1 - step, step)
+                        total = total + dense_buf[cell, pair, half, span, :]
+                        after = jnp.exp2(total * gate)
+                        weight = before - after
+                        before = after
+                        for channel in range(3):
+                            colour[channel] = colour[channel] + emitted_buf[channel, cell, pair, half, span, :].astype(jnp.float32) * weight
+                    for channel in range(3):
+                        out[pair, sub, channel] = colour[channel]
+                    out[pair, sub, 3] = before
+            return 0
+
+        lax.fori_loop(0, per, march_pair, 0)
         return 0
 
-    lax.fori_loop(0, pairs, march_pair, 0)
+    lax.fori_loop(0, chunks, march_chunk, 0)
 
 
-def march(dense, emitted, occupied, facing, other, bricks):
-    depth_len, pairs, _, rows, width = dense.shape
+def march(dense, emitted, occupied, facing, bricks):
+    _, pairs, _, rows, width = dense.shape
     tile_rows = pairs * 2 * rows // occupied.shape[0]
+    chunks = math.gcd(pairs, CHUNKS)
     hbm = pl.BlockSpec(memory_space=pl.ANY)
+    half = pltpu.VMEM((pairs, rows // ROWS, 4, ROWS, width), jnp.float32)
     return pl.pallas_call(
-        functools.partial(march_body, other=other, tile_rows=tile_rows, bricks=bricks),
+        functools.partial(march_body, chunks=chunks, tile_rows=tile_rows, bricks=bricks),
         in_specs=[pl.BlockSpec(memory_space=pltpu.SMEM), hbm, hbm, hbm],
-        out_specs=pl.BlockSpec(memory_space=pltpu.VMEM),
-        out_shape=pltpu.VMEM((pairs, rows // ROWS, 4, ROWS, width), jnp.float32),
+        out_specs=(pl.BlockSpec(memory_space=pltpu.VMEM), pl.BlockSpec(memory_space=pltpu.VMEM)),
+        out_shape=(half, half),
         scratch_shapes=[
-            pltpu.VMEM((depth_len, pairs, rows, width), jnp.float32),
-            pltpu.VMEM((3, depth_len, pairs, rows, width), jnp.bfloat16),
+            pltpu.VMEM(dense.shape, jnp.float32),
+            pltpu.VMEM(emitted.shape, jnp.bfloat16),
             pltpu.SMEM(occupied.shape, jnp.int32),
-            pltpu.SemaphoreType.DMA((pairs,)),
-            pltpu.SemaphoreType.DMA((pairs,)),
+            pltpu.SemaphoreType.DMA((chunks,)),
+            pltpu.SemaphoreType.DMA((chunks,)),
             pltpu.SemaphoreType.DMA,
         ],
         name="march",
@@ -126,8 +138,7 @@
     dense = density.reshape(depth_len, pairs, 2, unit, width)
     emitted = emission.reshape(3, depth_len, pairs, 2, unit, width)
 
-    give = march(dense, emitted, occupancy[0], facing, True, size)
-    keep = march(dense, emitted, occupancy[0], facing, False, size)
+    keep, give = march(dense, emitted, occupancy[0], facing, size)
     if not aligned:
         pair = jnp.arange(pairs)
         chosen = ((place & 1) ^ side(place >> 1)) ^ side(pair)
@@ -154,8 +165,8 @@
             keep, give_low = halves(mine, bit, place)
             give_high, give_both = halves(theirs, bit, place)
             got_both = swap(give_both, 3 * bit, size)
+            got_low = swap(give_low, bit, size)
             got_high = swap(give_high, 2 * bit, size)
-            got_low = swap(give_low, bit, size)
             value = over(over(keep, got_low, nearer(bit)), over(got_high, got_both, nearer(bit)), nearer(2 * bit))
             bit *= 4
         else:

time: 21.1 us -> 20.7 us (0.981)
  Pallas kernels: 4.08 us -> 2.78 us
  waiting for transfers between devices: 8.14 us -> 9.01 us
    pallas_call x2 -> x1, Pallas kernels: 4.08 us -> 2.78 us  [march(): pl.pallas_call(functools.partial(march_body, chunks=chunks, tile_rows=til...]
    ppermute x5, waiting for transfers between devices: 8.14 us -> 9.01 us  [swap(): return lax.ppermute(value, 'depth', [(i, i ^ mask) for i in range(size)])]
  transfers between devices with their start and end apart: 5 -> 5, of which waited for: 4 -> 5; matrix products, arithmetic and copies ran while one was open for 0% -> 0% of each run, Pallas kernels for 10% -> 0%
where the time goes in v3:
time: 20.7 us; the launch traced here: 20.5 us
  waiting for transfers between devices  9.01 us (44%)
  starting transfers between devices  7.19 us (35%)
  Pallas kernels  2.78 us (13%)
  other arithmetic  0.78 us (4%)
  between operations  0.71 us (3%)
    ppermute x5, waiting for transfers between devices, swap(): return lax.ppermute(value, 'depth', [(i, i ^ mask) for i in range(size)])  9.01 us
    ppermute x5, starting transfers between devices, swap(): return lax.ppermute(value, 'depth', [(i, i ^ mask) for i in range(size)])  7.19 us
    pallas_call x1, Pallas kernels, march(): pl.pallas_call(functools.partial(march_body, chunks=chunks, tile_rows=til...  2.78 us
    concatenate x1, other arithmetic, on_device(): return jnp.concatenate([value[:3], 1.0 - value[3:]], axis=0)  0.62 us
  transfers between devices with their start and end apart: 5, of which 5 were waited for; matrix products, arithmetic and copies ran while one was open for 0% of the time, Pallas kernels for 0%

profile of v3, /device:TPU:0, one launch (start us, length us, event | category | flops | bytes accessed | tf_op | source)
XLA Modules:
  0.0 20.5 jit_solution(7940792625993641464)
XLA Ops:
  0.7 2.8 %march.1 = (f32[8,1,4,8,256]{4,3,2,1,0:T(8,128)S(1)}, f32[8,1,4,8,256]{4,3,2,1,0:T(8,128)S(1)}) custom-call(s32[1]{0:T(128)S(6)} %copy.5.facing, s32[4,4]{1,0:T(4,128)} %bitcast.40, f32[16,8,2,8,256]{4,3,2,1,0:T(8,128)} %bitcast.38, bf16[3,16,8,2,8,256]{5,4,3,2,1,0:T(8,128)(2,1)} %bitcast.37), custom_call_target="tpu_custom_call" | custom-call | tf_op jit(solution)/shard_map/march/pallas_call | solution.py:95
  3.4 0.6 %collective-permute-start = (f32[8,1,4,8,256]{4,3,2,1,0:T(8,128)S(1)}, f32[8,1,4,8,256]{4,3,2,1,0:T(8,128)S(1)}, u32[]{:S(2)}, u32[]{:S(2)}) collective-permute-start(f32[8,1,4,8,256]{4,3,2,1,0:T(8,128)S(1)} %get-tuple-element.8), channel_id=1, source_target_pairs={{0,1},{1,0},{2,3},{3,2},{4,5},{5,4},{6,7},{7,6},{8,9},{9,8},{10,11... | collective-permute-start | bytes 786440 | tf_op jit(solution)/shard_map/ppermute | solution.py:121
  4.0 1.2 %collective-permute-done = f32[8,1,4,8,256]{4,3,2,1,0:T(8,128)S(1)} collective-permute-done((f32[8,1,4,8,256]{4,3,2,1,0:T(8,128)S(1)}, f32[8,1,4,8,256]{4,3,2,1,0:T(8,128)S(1)}, u32[]{:S(2)}, u32[]{:S(2)}) %collective-permute-start) | collective-permute-done | bytes 262176 | tf_op jit(solution)/shard_map/ppermute | solution.py:121
  5.3 2.7 %collective-permute-start.1 = (f32[2,1,4,8,256]{4,3,2,1,0:T(8,128)S(1)}, f32[2,1,4,8,256]{4,3,2,1,0:T(8,128)S(1)}, u32[]{:S(2)}, u32[]{:S(2)}) collective-permute-start(f32[2,1,4,8,256]{4,3,2,1,0:T(8,128)S(1)} %get-tuple-element.9), channel_id=1, source_target_pairs={{0,3},{1,2},{2,1},{3,0},{4,7},{5,6},{6,5},{7,4},{8,11},{9,10},{10,... | collective-permute-start | bytes 196616 | tf_op jit(solution)/shard_map/ppermute | solution.py:121
  8.0 1.6 %collective-permute-start.2 = (f32[2,1,4,8,256]{4,3,2,1,0:T(8,128)S(1)}, f32[2,1,4,8,256]{4,3,2,1,0:T(8,128)S(1)}, u32[]{:S(2)}, u32[]{:S(2)}) collective-permute-start(f32[2,1,4,8,256]{4,3,2,1,0:T(8,128)S(1)} %get-tuple-element.11), channel_id=1, source_target_pairs={{0,4},{1,5},{2,6},{3,7},{4,0},{5,1},{6,2},{7,3},{8,12},{9,13},{10,... | collective-permute-start | bytes 196616 | tf_op jit(solution)/shard_map/ppermute | solution.py:121
  9.6 0.0 collective-permute-start.3
  9.6 0.6 %collective-permute-done.1 = f32[2,1,4,8,256]{4,3,2,1,0:T(8,128)S(1)} collective-permute-done((f32[2,1,4,8,256]{4,3,2,1,0:T(8,128)S(1)}, f32[2,1,4,8,256]{4,3,2,1,0:T(8,128)S(1)}, u32[]{:S(2)}, u32[]{:S(2)}) %collective-permute-start.1) | collective-permute-done | bytes 65568 | tf_op jit(solution)/shard_map/ppermute | solution.py:121
  10.1 2.2 %collective-permute-done.2 = f32[2,1,4,8,256]{4,3,2,1,0:T(8,128)S(1)} collective-permute-done((f32[2,1,4,8,256]{4,3,2,1,0:T(8,128)S(1)}, f32[2,1,4,8,256]{4,3,2,1,0:T(8,128)S(1)}, u32[]{:S(2)}, u32[]{:S(2)}) %collective-permute-start.2) | collective-permute-done | bytes 65568 | tf_op jit(solution)/shard_map/ppermute | solution.py:121
  12.3 2.2 %collective-permute-done.3 = f32[2,1,4,8,256]{4,3,2,1,0:T(8,128)S(1)} collective-permute-done((f32[2,1,4,8,256]{4,3,2,1,0:T(8,128)S(1)}, f32[2,1,4,8,256]{4,3,2,1,0:T(8,128)S(1)}, u32[]{:S(2)}, u32[]{:S(2)}) %collective-permute-start.3) | collective-permute-done | bytes 65568 | tf_op jit(solution)/shard_map/ppermute | solution.py:121
  14.7 2.4 %collective-permute-start.4 = (f32[1,1,4,8,256]{4,3,2,1,0:T(8,128)S(1)}, f32[1,1,4,8,256]{4,3,2,1,0:T(8,128)S(1)}, u32[]{:S(2)}, u32[]{:S(2)}) collective-permute-start(f32[1,1,4,8,256]{4,3,2,1,0:T(8,128)S(1)} %get-tuple-element.20), channel_id=1, source_target_pairs={{0,9},{1,8},{2,11},{3,10},{4,13},{5,12},{6,15},{7,14},{8,1},{9,0},... | collective-permute-start | bytes 98312 | tf_op jit(solution)/shard_map/ppermute | solution.py:121
  17.0 2.8 %collective-permute-done.4 = f32[1,1,4,8,256]{4,3,2,1,0:T(8,128)S(1)} collective-permute-done((f32[1,1,4,8,256]{4,3,2,1,0:T(8,128)S(1)}, f32[1,1,4,8,256]{4,3,2,1,0:T(8,128)S(1)}, u32[]{:S(2)}, u32[]{:S(2)}) %collective-permute-start.4) | collective-permute-done | bytes 32800 | tf_op jit(solution)/shard_map/ppermute | solution.py:121
  19.9 0.6 %pad_maximum_fusion.1 = f32[4,8,256]{2,1,0:T(8,128)} fusion(f32[1,8,256]{2,1,0:T(8,128)S(1)} %get-tuple-element.26, f32[3,8,256]{2,1,0:T(8,128)S(1)} %select_bitcast_fusion), kind=kLoop, calls=%fused_computation.16 | loop fusion | flops 8192 | bytes 65536 | tf_op jit(solution)/shard_map/concatenate | solution.py:178
  (9 shorter events, 0.2 us)
Async XLA Ops:
  3.4 1.7 %collective-permute-start = (f32[8,1,4,8,256]{4,3,2,1,0:T(8,128)S(1)}, f32[8,1,4,8,256]{4,3,2,1,0:T(8,128)S(1)}, u32[]{:S(2)}, u32[]{:S(2)}) collective-permute-start(f32[8,1,4,8,256]{4,3,2,1,0:T(8,128)S(1)} %get-tuple-element.8), channel_id=1, source_target_pairs={{0,1},{1,0},{2,3},{3,2},{4,5},{5,4},{6,7},{7,6},{8,9},{9,8},{10,11... | collective-permute-start | bytes 786440 | tf_op jit(solution)/shard_map/ppermute | solution.py:121
  5.3 4.9 %collective-permute-start.1 = (f32[2,1,4,8,256]{4,3,2,1,0:T(8,128)S(1)}, f32[2,1,4,8,256]{4,3,2,1,0:T(8,128)S(1)}, u32[]{:S(2)}, u32[]{:S(2)}) collective-permute-start(f32[2,1,4,8,256]{4,3,2,1,0:T(8,128)S(1)} %get-tuple-element.9), channel_id=1, source_target_pairs={{0,3},{1,2},{2,1},{3,0},{4,7},{5,6},{6,5},{7,4},{8,11},{9,10},{10,... | collective-permute-start | bytes 196616 | tf_op jit(solution)/shard_map/ppermute | solution.py:121
  8.0 4.4 %collective-permute-start.2 = (f32[2,1,4,8,256]{4,3,2,1,0:T(8,128)S(1)}, f32[2,1,4,8,256]{4,3,2,1,0:T(8,128)S(1)}, u32[]{:S(2)}, u32[]{:S(2)}) collective-permute-start(f32[2,1,4,8,256]{4,3,2,1,0:T(8,128)S(1)} %get-tuple-element.11), channel_id=1, source_target_pairs={{0,4},{1,5},{2,6},{3,7},{4,0},{5,1},{6,2},{7,3},{8,12},{9,13},{10,... | collective-permute-start | bytes 196616 | tf_op jit(solution)/shard_map/ppermute | solution.py:121
  9.6 5.0 %collective-permute-start.3 = (f32[2,1,4,8,256]{4,3,2,1,0:T(8,128)S(1)}, f32[2,1,4,8,256]{4,3,2,1,0:T(8,128)S(1)}, u32[]{:S(2)}, u32[]{:S(2)}) collective-permute-start(f32[2,1,4,8,256]{4,3,2,1,0:T(8,128)S(1)} %get-tuple-element.10), channel_id=1, source_target_pairs={{0,7},{1,6},{2,5},{3,4},{4,3},{5,2},{6,1},{7,0},{8,15},{9,14},{10,... | collective-permute-start | bytes 196616 | tf_op jit(solution)/shard_map/ppermute | solution.py:121
  14.7 5.2 %collective-permute-start.4 = (f32[1,1,4,8,256]{4,3,2,1,0:T(8,128)S(1)}, f32[1,1,4,8,256]{4,3,2,1,0:T(8,128)S(1)}, u32[]{:S(2)}, u32[]{:S(2)}) collective-permute-start(f32[1,1,4,8,256]{4,3,2,1,0:T(8,128)S(1)} %get-tuple-element.20), channel_id=1, source_target_pairs={{0,9},{1,8},{2,11},{3,10},{4,13},{5,12},{6,15},{7,14},{8,1},{9,0},... | collective-permute-start | bytes 98312 | tf_op jit(solution)/shard_map/ppermute | solution.py:121

commit v4 on v3

v4 whole, which is shorter than its diff:
```python
import functools
import math

import jax
import jax.numpy as jnp
from jax import lax
from jax.experimental import pallas as pl
from jax.experimental.pallas import tpu as pltpu
from jax.sharding import PartitionSpec as P


ROWS = 8
CHUNKS = 8
CROSSING = 0xFFFE & ~4


def parity(bits):
    for shift in (8, 4, 2, 1):
        bits = bits ^ (bits >> shift)
    return bits & 1


def side(pair):
    return parity((pair * 2) & CROSSING)


def slot(pair, place, pairs):
    apart = pair ^ (place >> 1)
    quarter = pairs // 4
    return (apart & 3) * quarter + (apart >> 2) if quarter else apart


def march_body(facing, occupied_hbm, dense, emitted, keep, give, dense_buf, emitted_buf, occupied, dense_sem, emitted_sem, small_sem, *, chunks, tile_rows, bricks, ordered):
    depth_len, pairs, _, rows, width = dense.shape
    _, tiles_w = occupied.shape
    per = pairs // chunks
    place = lax.axis_index("depth")
    chosen = (place & 1) ^ side(place >> 1)

    small = pltpu.make_async_copy(occupied_hbm, occupied, small_sem)
    small.start()

    def copies(chunk):
        span = pl.ds(chunk * per, per)
        return (
            pltpu.make_async_copy(dense.at[:, span], dense_buf.at[:, span], dense_sem.at[chunk]),
            pltpu.make_async_copy(emitted.at[:, :, span], emitted_buf.at[:, :, span], emitted_sem.at[chunk]),
        )

    for chunk in range(chunks):
        for copy in copies(chunk):
            copy.start()

    lane = lax.broadcasted_iota(jnp.int32, (ROWS, width), 1) // (width // tiles_w)
    scale = -math.log2(math.e) / (depth_len * bricks)
    small.wait()
    backward = facing[0] != 0

    def march_chunk(chunk, _):
        for copy in copies(chunk):
            copy.wait()

        def march_pair(index, _):
            pair = chunk * per + index
            at = slot(pair, place, pairs) if ordered else pair
            for other, out in ((0, keep), (1, give)):
                half = chosen ^ side(pair) ^ other
                for sub in range(rows // ROWS):
                    tile = ((pair * 2 + half) * rows + sub * ROWS) // tile_rows
                    gate = jnp.zeros((ROWS, width), jnp.float32)
                    for column in range(tiles_w):
                        gate = jnp.where(lane == column, occupied[tile, column].astype(jnp.float32) * scale, gate)
                    span = pl.ds(sub * ROWS, ROWS)
                    total = jnp.zeros((ROWS, width), jnp.float32)
                    before = jnp.ones((ROWS, width), jnp.float32)
                    colour = [jnp.zeros((ROWS, width), jnp.float32) for _ in range(3)]
                    for step in range(depth_len):
                        cell = jnp.where(backward, depth_len - 1 - step, step)
                        total = total + dense_buf[cell, pair, half, span, :]
                        after = jnp.exp2(total * gate)
                        weight = before - after
                        before = after
                        for channel in range(3):
                            colour[channel] = colour[channel] + emitted_buf[channel, cell, pair, half, span, :].astype(jnp.float32) * weight
                    for channel in range(3):
                        out[at, sub, channel] = colour[channel]
                    out[at, sub, 3] = before
            return 0

        lax.fori_loop(0, per, march_pair, 0)
        return 0

    lax.fori_loop(0, chunks, march_chunk, 0)


def march(dense, emitted, occupied, facing, bricks, ordered):
    _, pairs, _, rows, width = dense.shape
    tile_rows = pairs * 2 * rows // occupied.shape[0]
    chunks = math.gcd(pairs, CHUNKS)
    hbm = pl.BlockSpec(memory_space=pl.ANY)
    half = pltpu.VMEM((pairs, rows // ROWS, 4, ROWS, width), jnp.float32)
    return pl.pallas_call(
        functools.partial(march_body, chunks=chunks, tile_rows=tile_rows, bricks=bricks, ordered=ordered),
        in_specs=[pl.BlockSpec(memory_space=pltpu.SMEM), hbm, hbm, hbm],
        out_specs=(pl.BlockSpec(memory_space=pltpu.VMEM), pl.BlockSpec(memory_space=pltpu.VMEM)),
        out_shape=(half, half),
        scratch_shapes=[
            pltpu.VMEM(dense.shape, jnp.float32),
            pltpu.VMEM(emitted.shape, jnp.bfloat16),
            pltpu.SMEM(occupied.shape, jnp.int32),
            pltpu.SemaphoreType.DMA((chunks,)),
            pltpu.SemaphoreType.DMA((chunks,)),
            pltpu.SemaphoreType.DMA,
        ],
        name="march",
    )(facing, occupied, dense, emitted)


def over(mine, other, nearer):
    near, far = jnp.where(nearer, mine, other), jnp.where(nearer, other, mine)
    through = near[3:]
    return jnp.concatenate([near[:3] + through * far[:3], through * far[3:]], axis=0)


def merge(body, facing, arrays, outs):
    def kernel(facing_ref, *refs):
        place = lax.axis_index("depth")
        forward = facing_ref[0] == 0
        body(lambda bit: ((place & bit) == 0) == forward, refs[: len(arrays)], refs[len(arrays) :])

    vmem = pl.BlockSpec(memory_space=pltpu.VMEM)
    return pl.pallas_call(
        kernel,
        in_specs=[pl.BlockSpec(memory_space=pltpu.SMEM)] + [vmem] * len(arrays),
        out_specs=[vmem] * len(outs),
        out_shape=outs,
    )(facing, *(pltpu.with_memory_space_constraint(array, pltpu.VMEM) for array in arrays))


def merge_cores(quarter, nearer, arrays, outs):
    keep, got = arrays
    for index, out in enumerate(outs):
        for k in range(quarter):
            for sub in range(keep.shape[1]):
                at = (index * quarter + k, sub)
                out[k, sub] = over(keep[at], got[at], nearer(1))


def merge_square(bit, nearer, arrays, outs):
    own, low, high, both = arrays
    for k, out in enumerate(outs):
        for sub in range(own.shape[1]):
            first = over(own[k, sub], low[k, sub], nearer(bit))
            second = over(high[k, sub], both[k, sub], nearer(bit))
            out[sub] = over(first, second, nearer(2 * bit))


def merge_pairs(bit, nearer, arrays, outs):
    for k, out in enumerate(outs):
        for sub in range(out.shape[0]):
            out[sub] = over(arrays[2 * k][sub], arrays[2 * k + 1][sub], nearer(bit))


def merge_last(bit, nearer, arrays, outs):
    mine, got = arrays
    for sub in range(mine.shape[0]):
        value = over(mine[sub], got[sub], nearer(bit))
        outs[0][:, pl.ds(sub * mine.shape[2], mine.shape[2]), :] = jnp.concatenate([value[:3], 1.0 - value[3:]], axis=0)


def swap(value, mask, size):
    mask = mask | parity(mask & CROSSING)
    return lax.ppermute(value, "depth", [(i, i ^ mask) for i in range(size)])


def on_device(density, emission, occupancy, facing):
    size = lax.axis_size("depth")
    place = lax.axis_index("depth")
    depth_len, height, width = density.shape
    rows = height // size
    aligned = rows % ROWS == 0
    pairs, unit = (size // 2, rows) if aligned else (height // (2 * ROWS), ROWS)
    dense = density.reshape(depth_len, pairs, 2, unit, width)
    emitted = emission.reshape(3, depth_len, pairs, 2, unit, width)

    keep, give = march(dense, emitted, occupancy[0], facing, size, aligned)
    if not aligned:
        chosen = (place & 1) ^ side(place >> 1)
        pair = jnp.arange(pairs)
        swapped = ((chosen ^ side(pair)) == 1)[:, None, None, None]
        both = jnp.stack([jnp.where(swapped, give[:, 0], keep[:, 0]), jnp.where(swapped, keep[:, 0], give[:, 0])], axis=1)
        pairs = size // 2
        both = jnp.moveaxis(both, 2, 0).reshape(4, pairs, 2, 1, rows, width)
        both = jnp.moveaxis(both, 0, 3)
        pair = jnp.arange(pairs)
        swapped = ((chosen ^ side(pair)) == 1)[:, None, None, None, None]
        order = jnp.zeros((pairs,), jnp.int32).at[slot(pair, place, pairs)].set(pair)
        keep = jnp.where(swapped, both[:, 1], both[:, 0])[order]
        give = jnp.where(swapped, both[:, 0], both[:, 1])[order]
    got = swap(give, 1, size)
    tile = keep.shape[1:]
    quarter = pairs // 4
    group = pltpu.VMEM((quarter,) + tile, jnp.float32)
    own, low, high, both = merge(functools.partial(merge_cores, quarter), facing, (keep, got), [group] * 4)
    got_both = swap(both, 6, size)
    got_low = swap(low, 2, size)
    got_high = swap(high, 4, size)
    one = pltpu.VMEM(tile, jnp.float32)
    mine = merge(functools.partial(merge_square, 2), facing, (own, got_low, got_high, got_both), [one] * quarter)
    bit = 8
    while 2 * bit < size:
        both = [part for k in range(0, len(mine), 2) for part in (mine[k], swap(mine[k + 1], bit, size))]
        mine = merge(functools.partial(merge_pairs, bit), facing, both, [one] * (len(mine) // 2))
        bit *= 2
    image = jax.ShapeDtypeStruct((4, rows, width), jnp.float32)
    return merge(functools.partial(merge_last, bit), facing, (mine[0], swap(mine[1], bit, size)), [image])[0]


def solution(mesh):
    return jax.shard_map(
        on_device,
        mesh=mesh,
        in_specs=(
            P(("views", "depth"), None, None),
            P("views", "depth", None, None),
            P(("views", "depth"), None, None),
            P("views"),
        ),
        out_specs=P("views", "depth", None),
        check_vma=False,
    )
```

time: 20.7 us -> 20.5 us (level)
  other arithmetic: 0.78 us -> 0 us
  Pallas kernels: 2.78 us -> 3.48 us
    pallas_call x0 -> x3, Pallas kernels: none -> 0.7 us  [merge(): pl.pallas_call(kernel, in_specs=[pl.BlockSpec(memory_space=pltpu.SMEM)] +...]
    concatenate x3 -> x0, other arithmetic: 0.66 us -> none  [the longest x1 0.62 us: on_device(): return jnp.concatenate([value[:3], 1.0 - value[3:]], axis=0)]
where the time goes in v4:
time: 20.5 us; the launch traced here: 20.4 us
  waiting for transfers between devices  9.01 us (44%)
  starting transfers between devices  7.19 us (35%)
  Pallas kernels  3.48 us (17%)
  between operations  0.67 us (3%)
    ppermute x5, waiting for transfers between devices, swap(): return lax.ppermute(value, 'depth', [(i, i ^ mask) for i in range(size)])  9.01 us
    ppermute x5, starting transfers between devices, swap(): return lax.ppermute(value, 'depth', [(i, i ^ mask) for i in range(size)])  7.19 us
    pallas_call x1, Pallas kernels, march(): pl.pallas_call(functools.partial(march_body, chunks=chunks, tile_rows=til...  2.77 us
    pallas_call x3, Pallas kernels, merge(): pl.pallas_call(kernel, in_specs=[pl.BlockSpec(memory_space=pltpu.SMEM)] +...  0.7 us
  transfers between devices with their start and end apart: 5, of which 5 were waited for; matrix products, arithmetic and copies ran while one was open for 0% of the time, Pallas kernels for 0%

profile of v4, /device:TPU:0, one launch (start us, length us, event | category | flops | bytes accessed | tf_op | source)
XLA Modules:
  0.0 20.4 jit_solution(11193987888542773506)
XLA Ops:
  0.7 2.8 %march.1 = (f32[8,1,4,8,256]{4,3,2,1,0:T(8,128)S(1)}, f32[8,1,4,8,256]{4,3,2,1,0:T(8,128)S(1)}) custom-call(s32[1]{0:T(128)S(6)} %copy.5.facing.facing_ref, s32[4,4]{1,0:T(4,128)} %bitcast.5, f32[16,8,2,8,256]{4,3,2,1,0:T(8,128)} %bitcast.4, bf16[3,16,8,2,8,256]{5,4,3,2,1,0:T(8,128)(2,1)} %bitcast.3), custom_call_target="tpu_custom_call" | custom-call | tf_op jit(solution)/shard_map/march/pallas_call | solution.py:102
  3.4 0.6 %collective-permute-start = (f32[8,1,4,8,256]{4,3,2,1,0:T(8,128)S(1)}, f32[8,1,4,8,256]{4,3,2,1,0:T(8,128)S(1)}, u32[]{:S(2)}, u32[]{:S(2)}) collective-permute-start(f32[8,1,4,8,256]{4,3,2,1,0:T(8,128)S(1)} %get-tuple-element.14), channel_id=1, source_target_pairs={{0,1},{1,0},{2,3},{3,2},{4,5},{5,4},{6,7},{7,6},{8,9},{9,8},{10,11... | collective-permute-start | bytes 786440 | tf_op jit(solution)/shard_map/ppermute | solution.py:173
  4.0 1.2 %collective-permute-done.refs_1_ = f32[8,1,4,8,256]{4,3,2,1,0:T(8,128)S(1)} collective-permute-done((f32[8,1,4,8,256]{4,3,2,1,0:T(8,128)S(1)}, f32[8,1,4,8,256]{4,3,2,1,0:T(8,128)S(1)}, u32[]{:S(2)}, u32[]{:S(2)}) %collective-permute-start) | collective-permute-done | bytes 262176 | tf_op jit(solution)/shard_map/ppermute | solution.py:173
  5.2 2.7 %collective-permute-start.1 = (f32[2,1,4,8,256]{4,3,2,1,0:T(8,128)S(1)}, f32[2,1,4,8,256]{4,3,2,1,0:T(8,128)S(1)}, u32[]{:S(2)}, u32[]{:S(2)}) collective-permute-start(f32[2,1,4,8,256]{4,3,2,1,0:T(8,128)S(1)} %get-tuple-element.16), channel_id=1, source_target_pairs={{0,3},{1,2},{2,1},{3,0},{4,7},{5,6},{6,5},{7,4},{8,11},{9,10},{10,... | collective-permute-start | bytes 196616 | tf_op jit(solution)/shard_map/ppermute | solution.py:173
  7.9 1.6 %collective-permute-start.2 = (f32[2,1,4,8,256]{4,3,2,1,0:T(8,128)S(1)}, f32[2,1,4,8,256]{4,3,2,1,0:T(8,128)S(1)}, u32[]{:S(2)}, u32[]{:S(2)}) collective-permute-start(f32[2,1,4,8,256]{4,3,2,1,0:T(8,128)S(1)} %get-tuple-element.17), channel_id=1, source_target_pairs={{0,4},{1,5},{2,6},{3,7},{4,0},{5,1},{6,2},{7,3},{8,12},{9,13},{10,... | collective-permute-start | bytes 196616 | tf_op jit(solution)/shard_map/ppermute | solution.py:173
  9.5 0.0 collective-permute-start.3
  9.5 0.6 %collective-permute-done.1.refs_1_ = f32[2,1,4,8,256]{4,3,2,1,0:T(8,128)S(1)} collective-permute-done((f32[2,1,4,8,256]{4,3,2,1,0:T(8,128)S(1)}, f32[2,1,4,8,256]{4,3,2,1,0:T(8,128)S(1)}, u32[]{:S(2)}, u32[]{:S(2)}) %collective-permute-start.1) | collective-permute-done | bytes 65568 | tf_op jit(solution)/shard_map/ppermute | solution.py:173
  10.1 2.2 %collective-permute-done.2.refs_2_ = f32[2,1,4,8,256]{4,3,2,1,0:T(8,128)S(1)} collective-permute-done((f32[2,1,4,8,256]{4,3,2,1,0:T(8,128)S(1)}, f32[2,1,4,8,256]{4,3,2,1,0:T(8,128)S(1)}, u32[]{:S(2)}, u32[]{:S(2)}) %collective-permute-start.2) | collective-permute-done | bytes 65568 | tf_op jit(solution)/shard_map/ppermute | solution.py:173
  12.3 2.2 %collective-permute-done.3.refs_3_ = f32[2,1,4,8,256]{4,3,2,1,0:T(8,128)S(1)} collective-permute-done((f32[2,1,4,8,256]{4,3,2,1,0:T(8,128)S(1)}, f32[2,1,4,8,256]{4,3,2,1,0:T(8,128)S(1)}, u32[]{:S(2)}, u32[]{:S(2)}) %collective-permute-start.3) | collective-permute-done | bytes 65568 | tf_op jit(solution)/shard_map/ppermute | solution.py:173
  14.5 2.4 %collective-permute-start.4 = (f32[1,4,8,256]{3,2,1,0:T(8,128)S(1)}, f32[1,4,8,256]{3,2,1,0:T(8,128)S(1)}, u32[]{:S(2)}, u32[]{:S(2)}) collective-permute-start(f32[1,4,8,256]{3,2,1,0:T(8,128)S(1)} %get-tuple-element.20), channel_id=1, source_target_pairs={{0,9},{1,8},{2,11},{3,10},{4,13},{5,12},{6,15},{7,14},{8,1},{9,0},... | collective-permute-start | bytes 98312 | tf_op jit(solution)/shard_map/ppermute | solution.py:173
  16.9 2.8 %collective-permute-done.4.refs_1_ = f32[1,4,8,256]{3,2,1,0:T(8,128)S(1)} collective-permute-done((f32[1,4,8,256]{3,2,1,0:T(8,128)S(1)}, f32[1,4,8,256]{3,2,1,0:T(8,128)S(1)}, u32[]{:S(2)}, u32[]{:S(2)}) %collective-permute-start.4) | collective-permute-done | bytes 32800 | tf_op jit(solution)/shard_map/ppermute | solution.py:173
  19.7 0.6 %shard_map.48 = f32[4,8,256]{2,1,0:T(8,128)} custom-call(s32[1]{0:T(128)S(6)} %copy.5.facing.facing_ref, f32[1,4,8,256]{3,2,1,0:T(8,128)S(1)} %get-tuple-element.19.refs_0_, f32[1,4,8,256]{3,2,1,0:T(8,128)S(1)} %collective-permute-done.4.refs_1_), custom_call_target="tpu_custom_call" | custom-call | tf_op jit(solution)/shard_map/pallas_call | solution.py:132
  (2 shorter events, 0.1 us)
Async XLA Ops:
  3.4 1.7 %collective-permute-start = (f32[8,1,4,8,256]{4,3,2,1,0:T(8,128)S(1)}, f32[8,1,4,8,256]{4,3,2,1,0:T(8,128)S(1)}, u32[]{:S(2)}, u32[]{:S(2)}) collective-permute-start(f32[8,1,4,8,256]{4,3,2,1,0:T(8,128)S(1)} %get-tuple-element.14), channel_id=1, source_target_pairs={{0,1},{1,0},{2,3},{3,2},{4,5},{5,4},{6,7},{7,6},{8,9},{9,8},{10,11... | collective-permute-start | bytes 786440 | tf_op jit(solution)/shard_map/ppermute | solution.py:173
  5.2 4.9 %collective-permute-start.1 = (f32[2,1,4,8,256]{4,3,2,1,0:T(8,128)S(1)}, f32[2,1,4,8,256]{4,3,2,1,0:T(8,128)S(1)}, u32[]{:S(2)}, u32[]{:S(2)}) collective-permute-start(f32[2,1,4,8,256]{4,3,2,1,0:T(8,128)S(1)} %get-tuple-element.16), channel_id=1, source_target_pairs={{0,3},{1,2},{2,1},{3,0},{4,7},{5,6},{6,5},{7,4},{8,11},{9,10},{10,... | collective-permute-start | bytes 196616 | tf_op jit(solution)/shard_map/ppermute | solution.py:173
  7.9 4.4 %collective-permute-start.2 = (f32[2,1,4,8,256]{4,3,2,1,0:T(8,128)S(1)}, f32[2,1,4,8,256]{4,3,2,1,0:T(8,128)S(1)}, u32[]{:S(2)}, u32[]{:S(2)}) collective-permute-start(f32[2,1,4,8,256]{4,3,2,1,0:T(8,128)S(1)} %get-tuple-element.17), channel_id=1, source_target_pairs={{0,4},{1,5},{2,6},{3,7},{4,0},{5,1},{6,2},{7,3},{8,12},{9,13},{10,... | collective-permute-start | bytes 196616 | tf_op jit(solution)/shard_map/ppermute | solution.py:173
  9.5 5.0 %collective-permute-start.3 = (f32[2,1,4,8,256]{4,3,2,1,0:T(8,128)S(1)}, f32[2,1,4,8,256]{4,3,2,1,0:T(8,128)S(1)}, u32[]{:S(2)}, u32[]{:S(2)}) collective-permute-start(f32[2,1,4,8,256]{4,3,2,1,0:T(8,128)S(1)} %get-tuple-element.18), channel_id=1, source_target_pairs={{0,7},{1,6},{2,5},{3,4},{4,3},{5,2},{6,1},{7,0},{8,15},{9,14},{10,... | collective-permute-start | bytes 196616 | tf_op jit(solution)/shard_map/ppermute | solution.py:173
  14.5 5.2 %collective-permute-start.4 = (f32[1,4,8,256]{3,2,1,0:T(8,128)S(1)}, f32[1,4,8,256]{3,2,1,0:T(8,128)S(1)}, u32[]{:S(2)}, u32[]{:S(2)}) collective-permute-start(f32[1,4,8,256]{3,2,1,0:T(8,128)S(1)} %get-tuple-element.20), channel_id=1, source_target_pairs={{0,9},{1,8},{2,11},{3,10},{4,13},{5,12},{6,15},{7,14},{8,1},{9,0},... | collective-permute-start | bytes 98312 | tf_op jit(solution)/shard_map/ppermute | solution.py:173

commit v5 on v4

--- a/solution.py
+++ b/solution.py
@@ -11,6 +11,8 @@
 
 ROWS = 8
 CHUNKS = 8
+SPLIT = ('low', 'high')
+ORDER = ('both', 'higha', 'lowa', 'lowb', 'highb')
 CROSSING = 0xFFFE & ~4
 
 
@@ -137,22 +139,21 @@
     )(facing, *(pltpu.with_memory_space_constraint(array, pltpu.VMEM) for array in arrays))
 
 
-def merge_cores(quarter, nearer, arrays, outs):
+def merge_cores(groups, nearer, arrays, outs):
     keep, got = arrays
-    for index, out in enumerate(outs):
-        for k in range(quarter):
+    for group, out in zip(groups, outs):
+        for k, at in enumerate(group):
             for sub in range(keep.shape[1]):
-                at = (index * quarter + k, sub)
-                out[k, sub] = over(keep[at], got[at], nearer(1))
+                out[k, sub] = over(keep[at, sub], got[at, sub], nearer(1))
 
 
 def merge_square(bit, nearer, arrays, outs):
-    own, low, high, both = arrays
     for k, out in enumerate(outs):
-        for sub in range(own.shape[1]):
-            first = over(own[k, sub], low[k, sub], nearer(bit))
-            second = over(high[k, sub], both[k, sub], nearer(bit))
-            out[sub] = over(first, second, nearer(2 * bit))
+        own, low, high, both = ((ref, at) for ref, at in zip(arrays, bit[1][k]))
+        for sub in range(out.shape[0]):
+            first = over(own[0][own[1], sub], low[0][low[1], sub], nearer(bit[0]))
+            second = over(high[0][high[1], sub], both[0][both[1], sub], nearer(bit[0]))
+            out[sub] = over(first, second, nearer(2 * bit[0]))
 
 
 def merge_pairs(bit, nearer, arrays, outs):
@@ -200,20 +201,34 @@
     got = swap(give, 1, size)
     tile = keep.shape[1:]
     quarter = pairs // 4
-    group = pltpu.VMEM((quarter,) + tile, jnp.float32)
-    own, low, high, both = merge(functools.partial(merge_cores, quarter), facing, (keep, got), [group] * 4)
-    got_both = swap(both, 6, size)
-    got_low = swap(low, 2, size)
-    got_high = swap(high, 4, size)
+    later, sooner = list(range(0, quarter, 2)), list(range(1, quarter, 2))
+    groups = {}
+    for index, name in enumerate(("own", "low", "high", "both")):
+        for part, members in (("a", sooner), ("b", later)) if name in SPLIT else (("", sooner + later),):
+            groups[name + part] = [index * quarter + k for k in members]
+    shapes = [pltpu.VMEM((len(group),) + tile, jnp.float32) for group in groups.values()]
+    parts = merge(functools.partial(merge_cores, list(groups.values())), facing, (keep, got), shapes)
+    parts = dict(zip(groups, parts))
+    arrived = {"own": parts["own"]}
+    for name in ORDER:
+        arrived[name] = swap(parts[name], {"low": 2, "high": 4, "both": 6}[name.rstrip("ab") if name != "both" else name], size)
     one = pltpu.VMEM(tile, jnp.float32)
-    mine = merge(functools.partial(merge_square, 2), facing, (own, got_low, got_high, got_both), [one] * quarter)
+
+    def square(members, part):
+        names = [name + (part if name in SPLIT else "") for name in ("own", "low", "high", "both")]
+        places = [[groups[name].index(index * quarter + k) for index, name in enumerate(names)] for k in members]
+        return merge(functools.partial(merge_square, (2, places)), facing, [arrived[name] for name in names], [one] * len(members))
+
+    going, staying = square(sooner, "a"), square(later, "b")
+    mine = [part for pair in zip(staying, going) for part in pair]
     bit = 8
     while 2 * bit < size:
         both = [part for k in range(0, len(mine), 2) for part in (mine[k], swap(mine[k + 1], bit, size))]
         mine = merge(functools.partial(merge_pairs, bit), facing, both, [one] * (len(mine) // 2))
         bit *= 2
     image = jax.ShapeDtypeStruct((4, rows, width), jnp.float32)
-    return merge(functools.partial(merge_last, bit), facing, (mine[0], swap(mine[1], bit, size)), [image])[0]
+    got = swap(mine[1], bit, size)
+    return merge(functools.partial(merge_last, bit), facing, (mine[0], got), [image])[0]
 
 
 def solution(mesh):

time: 20.5 us -> 18.8 us (0.917)
  the two profiles are of different devices: /device:TPU:0 before, /device:TPU:1 now
where the time goes in v5:
time: 18.8 us; the launch traced here: 18.6 us
  starting transfers between devices  10.2 us (54%)
  waiting for transfers between devices  4.3 us (23%)
  Pallas kernels  3.49 us (19%)
  between operations  0.69 us (4%)
    ppermute x7, starting transfers between devices, swap(): return lax.ppermute(value, 'depth', [(i, i ^ mask) for i in range(size)])  10.2 us
    ppermute x7, waiting for transfers between devices, swap(): return lax.ppermute(value, 'depth', [(i, i ^ mask) for i in range(size)])  4.3 us
    pallas_call x1, Pallas kernels, march(): pl.pallas_call(functools.partial(march_body, chunks=chunks, tile_rows=til...  2.77 us
    pallas_call x4, Pallas kernels, merge(): pl.pallas_call(kernel, in_specs=[pl.BlockSpec(memory_space=pltpu.SMEM)] +...  0.72 us
  transfers between devices with their start and end apart: 7, of which 3 were waited for; matrix products, arithmetic and copies ran while one was open for 0% of the time, Pallas kernels for 0%

profile of v5, /device:TPU:1, one launch (start us, length us, event | category | flops | bytes accessed | tf_op | source)
XLA Modules:
  0.0 18.6 jit_solution(5487836217070902677)
XLA Ops:
  0.7 2.8 %march.1 = (f32[8,1,4,8,256]{4,3,2,1,0:T(8,128)S(1)}, f32[8,1,4,8,256]{4,3,2,1,0:T(8,128)S(1)}) custom-call(s32[1]{0:T(128)S(6)} %copy.5.facing.facing_ref, s32[4,4]{1,0:T(4,128)} %bitcast.5, f32[16,8,2,8,256]{4,3,2,1,0:T(8,128)} %bitcast.4, bf16[3,16,8,2,8,256]{5,4,3,2,1,0:T(8,128)(2,1)} %bitcast.3), custom_call_target="tpu_custom_call" | custom-call | tf_op jit(solution)/shard_map/march/pallas_call | solution.py:104
  3.4 0.1 collective-permute-start
  3.5 1.5 %collective-permute-done.refs_1_ = f32[8,1,4,8,256]{4,3,2,1,0:T(8,128)S(1)} collective-permute-done((f32[8,1,4,8,256]{4,3,2,1,0:T(8,128)S(1)}, f32[8,1,4,8,256]{4,3,2,1,0:T(8,128)S(1)}, u32[]{:S(2)}, u32[]{:S(2)}) %collective-permute-start) | collective-permute-done | bytes 262176 | tf_op jit(solution)/shard_map/ppermute | solution.py:174
  5.1 3.7 %collective-permute-start.3 = (f32[2,1,4,8,256]{4,3,2,1,0:T(8,128)S(1)}, f32[2,1,4,8,256]{4,3,2,1,0:T(8,128)S(1)}, u32[]{:S(2)}, u32[]{:S(2)}) collective-permute-start(f32[2,1,4,8,256]{4,3,2,1,0:T(8,128)S(1)} %get-tuple-element.18), channel_id=1, source_target_pairs={{0,7},{1,6},{2,5},{3,4},{4,3},{5,2},{6,1},{7,0},{8,15},{9,14},{10,... | collective-permute-start | bytes 196616 | tf_op jit(solution)/shard_map/ppermute | solution.py:174
  8.8 0.2 %collective-permute-start.4 = (f32[1,1,4,8,256]{4,3,2,1,0:T(8,128)S(1)}, f32[1,1,4,8,256]{4,3,2,1,0:T(8,128)S(1)}, u32[]{:S(2)}, u32[]{:S(2)}) collective-permute-start(f32[1,1,4,8,256]{4,3,2,1,0:T(8,128)S(1)} %get-tuple-element.19), channel_id=1, source_target_pairs={{0,3},{1,2},{2,1},{3,0},{4,7},{5,6},{6,5},{7,4},{8,11},{9,10},{10,... | collective-permute-start | bytes 98312 | tf_op jit(solution)/shard_map/ppermute | solution.py:174
  9.0 0.1 collective-permute-start.5
  9.1 1.8 %collective-permute-start.1 = (f32[1,1,4,8,256]{4,3,2,1,0:T(8,128)S(1)}, f32[1,1,4,8,256]{4,3,2,1,0:T(8,128)S(1)}, u32[]{:S(2)}, u32[]{:S(2)}) collective-permute-start(f32[1,1,4,8,256]{4,3,2,1,0:T(8,128)S(1)} %get-tuple-element.16), channel_id=1, source_target_pairs={{0,3},{1,2},{2,1},{3,0},{4,7},{5,6},{6,5},{7,4},{8,11},{9,10},{10,... | collective-permute-start | bytes 98312 | tf_op jit(solution)/shard_map/ppermute | solution.py:174
  11.0 1.3 %collective-permute-start.2 = (f32[1,1,4,8,256]{4,3,2,1,0:T(8,128)S(1)}, f32[1,1,4,8,256]{4,3,2,1,0:T(8,128)S(1)}, u32[]{:S(2)}, u32[]{:S(2)}) collective-permute-start(f32[1,1,4,8,256]{4,3,2,1,0:T(8,128)S(1)} %get-tuple-element.17), channel_id=1, source_target_pairs={{0,4},{1,5},{2,6},{3,7},{4,0},{5,1},{6,2},{7,3},{8,12},{9,13},{10,... | collective-permute-start | bytes 98312 | tf_op jit(solution)/shard_map/ppermute | solution.py:174
  12.3 0.4 %collective-permute-done.4.refs_1_ = f32[1,1,4,8,256]{4,3,2,1,0:T(8,128)S(1)} collective-permute-done((f32[1,1,4,8,256]{4,3,2,1,0:T(8,128)S(1)}, f32[1,1,4,8,256]{4,3,2,1,0:T(8,128)S(1)}, u32[]{:S(2)}, u32[]{:S(2)}) %collective-permute-start.4) | collective-permute-done | bytes 32800 | tf_op jit(solution)/shard_map/ppermute | solution.py:174
  12.7 0.0 collective-permute-done.5.refs_2_
  12.7 0.0 collective-permute-done.3.refs_3_
  12.7 2.9 %collective-permute-start.6 = (f32[1,4,8,256]{3,2,1,0:T(8,128)S(1)}, f32[1,4,8,256]{3,2,1,0:T(8,128)S(1)}, u32[]{:S(2)}, u32[]{:S(2)}) collective-permute-start(f32[1,4,8,256]{3,2,1,0:T(8,128)S(1)} %shard_map.48), channel_id=1, source_target_pairs={{0,9},{1,8},{2,11},{3,10},{4,13},{5,12},{6,15},{7,14},{8,1},{9,0},... | collective-permute-start | bytes 98312 | tf_op jit(solution)/shard_map/ppermute | solution.py:174
  15.6 0.0 collective-permute-done.1.refs_1_
  15.6 0.0 collective-permute-done.2.refs_2_
  15.6 2.4 %collective-permute-done.6.refs_1_ = f32[1,4,8,256]{3,2,1,0:T(8,128)S(1)} collective-permute-done((f32[1,4,8,256]{3,2,1,0:T(8,128)S(1)}, f32[1,4,8,256]{3,2,1,0:T(8,128)S(1)}, u32[]{:S(2)}, u32[]{:S(2)}) %collective-permute-start.6) | collective-permute-done | bytes 32800 | tf_op jit(solution)/shard_map/ppermute | solution.py:174
  18.0 0.6 %shard_map.49 = f32[4,8,256]{2,1,0:T(8,128)} custom-call(s32[1]{0:T(128)S(6)} %copy.5.facing.facing_ref, f32[1,4,8,256]{3,2,1,0:T(8,128)S(1)} %shard_map.47.refs_0_, f32[1,4,8,256]{3,2,1,0:T(8,128)S(1)} %collective-permute-done.6.refs_1_), custom_call_target="tpu_custom_call" | custom-call | tf_op jit(solution)/shard_map/pallas_call | solution.py:134
  (3 shorter events, 0.1 us)
Async XLA Ops:
  3.4 1.6 %collective-permute-start = (f32[8,1,4,8,256]{4,3,2,1,0:T(8,128)S(1)}, f32[8,1,4,8,256]{4,3,2,1,0:T(8,128)S(1)}, u32[]{:S(2)}, u32[]{:S(2)}) collective-permute-start(f32[8,1,4,8,256]{4,3,2,1,0:T(8,128)S(1)} %get-tuple-element.14), channel_id=1, source_target_pairs={{0,1},{1,0},{2,3},{3,2},{4,5},{5,4},{6,7},{7,6},{8,9},{9,8},{10,11... | collective-permute-start | bytes 786440 | tf_op jit(solution)/shard_map/ppermute | solution.py:174
  5.1 7.6 %collective-permute-start.3 = (f32[2,1,4,8,256]{4,3,2,1,0:T(8,128)S(1)}, f32[2,1,4,8,256]{4,3,2,1,0:T(8,128)S(1)}, u32[]{:S(2)}, u32[]{:S(2)}) collective-permute-start(f32[2,1,4,8,256]{4,3,2,1,0:T(8,128)S(1)} %get-tuple-element.18), channel_id=1, source_target_pairs={{0,7},{1,6},{2,5},{3,4},{4,3},{5,2},{6,1},{7,0},{8,15},{9,14},{10,... | collective-permute-start | bytes 196616 | tf_op jit(solution)/shard_map/ppermute | solution.py:174
  8.8 3.9 %collective-permute-start.4 = (f32[1,1,4,8,256]{4,3,2,1,0:T(8,128)S(1)}, f32[1,1,4,8,256]{4,3,2,1,0:T(8,128)S(1)}, u32[]{:S(2)}, u32[]{:S(2)}) collective-permute-start(f32[1,1,4,8,256]{4,3,2,1,0:T(8,128)S(1)} %get-tuple-element.19), channel_id=1, source_target_pairs={{0,3},{1,2},{2,1},{3,0},{4,7},{5,6},{6,5},{7,4},{8,11},{9,10},{10,... | collective-permute-start | bytes 98312 | tf_op jit(solution)/shard_map/ppermute | solution.py:174
  9.0 3.6 %collective-permute-start.5 = (f32[1,1,4,8,256]{4,3,2,1,0:T(8,128)S(1)}, f32[1,1,4,8,256]{4,3,2,1,0:T(8,128)S(1)}, u32[]{:S(2)}, u32[]{:S(2)}) collective-permute-start(f32[1,1,4,8,256]{4,3,2,1,0:T(8,128)S(1)} %get-tuple-element.20), channel_id=1, source_target_pairs={{0,4},{1,5},{2,6},{3,7},{4,0},{5,1},{6,2},{7,3},{8,12},{9,13},{10,... | collective-permute-start | bytes 98312 | tf_op jit(solution)/shard_map/ppermute | solution.py:174
  9.1 6.5 %collective-permute-start.1 = (f32[1,1,4,8,256]{4,3,2,1,0:T(8,128)S(1)}, f32[1,1,4,8,256]{4,3,2,1,0:T(8,128)S(1)}, u32[]{:S(2)}, u32[]{:S(2)}) collective-permute-start(f32[1,1,4,8,256]{4,3,2,1,0:T(8,128)S(1)} %get-tuple-element.16), channel_id=1, source_target_pairs={{0,3},{1,2},{2,1},{3,0},{4,7},{5,6},{6,5},{7,4},{8,11},{9,10},{10,... | collective-permute-start | bytes 98312 | tf_op jit(solution)/shard_map/ppermute | solution.py:174
  11.0 4.6 %collective-permute-start.2 = (f32[1,1,4,8,256]{4,3,2,1,0:T(8,128)S(1)}, f32[1,1,4,8,256]{4,3,2,1,0:T(8,128)S(1)}, u32[]{:S(2)}, u32[]{:S(2)}) collective-permute-start(f32[1,1,4,8,256]{4,3,2,1,0:T(8,128)S(1)} %get-tuple-element.17), channel_id=1, source_target_pairs={{0,4},{1,5},{2,6},{3,7},{4,0},{5,1},{6,2},{7,3},{8,12},{9,13},{10,... | collective-permute-start | bytes 98312 | tf_op jit(solution)/shard_map/ppermute | solution.py:174
  12.7 5.3 %collective-permute-start.6 = (f32[1,4,8,256]{3,2,1,0:T(8,128)S(1)}, f32[1,4,8,256]{3,2,1,0:T(8,128)S(1)}, u32[]{:S(2)}, u32[]{:S(2)}) collective-permute-start(f32[1,4,8,256]{3,2,1,0:T(8,128)S(1)} %shard_map.48), channel_id=1, source_target_pairs={{0,9},{1,8},{2,11},{3,10},{4,13},{5,12},{6,15},{7,14},{8,1},{9,0},... | collective-permute-start | bytes 98312 | tf_op jit(solution)/shard_map/ppermute | solution.py:174

commit v6 on v5

--- a/solution.py
+++ b/solution.py
@@ -10,7 +10,8 @@
 
 
 ROWS = 8
-CHUNKS = 8
+LANES = 128
+BOUNDS = (0, 1, 2, 3, 4, 5, 6, 7, 8)
 SPLIT = ('low', 'high')
 ORDER = ('both', 'higha', 'lowa', 'lowb', 'highb')
 CROSSING = 0xFFFE & ~4
@@ -32,10 +33,9 @@
     return (apart & 3) * quarter + (apart >> 2) if quarter else apart
 
 
-def march_body(facing, occupied_hbm, dense, emitted, keep, give, dense_buf, emitted_buf, occupied, dense_sem, emitted_sem, small_sem, *, chunks, tile_rows, bricks, ordered):
+def march_body(occupied_hbm, dense, emitted, keep, give, dense_buf, emitted_buf, occupied, dense_sem, emitted_sem, small_sem, *, bounds, tile_rows, bricks, ordered):
     depth_len, pairs, _, rows, width = dense.shape
     _, tiles_w = occupied.shape
-    per = pairs // chunks
     place = lax.axis_index("depth")
     chosen = (place & 1) ^ side(place >> 1)
 
@@ -43,67 +43,72 @@
     small.start()
 
     def copies(chunk):
-        span = pl.ds(chunk * per, per)
+        span = pl.ds(bounds[chunk], bounds[chunk + 1] - bounds[chunk])
         return (
             pltpu.make_async_copy(dense.at[:, span], dense_buf.at[:, span], dense_sem.at[chunk]),
             pltpu.make_async_copy(emitted.at[:, :, span], emitted_buf.at[:, :, span], emitted_sem.at[chunk]),
         )
 
-    for chunk in range(chunks):
+    for chunk in range(len(bounds) - 1):
         for copy in copies(chunk):
             copy.start()
 
     lane = lax.broadcasted_iota(jnp.int32, (ROWS, width), 1) // (width // tiles_w)
     scale = -math.log2(math.e) / (depth_len * bricks)
     small.wait()
-    backward = facing[0] != 0
-
-    def march_chunk(chunk, _):
+
+    def march_tile(pair, other, out):
+        at = slot(pair, place, pairs) if ordered else pair
+        half = chosen ^ side(pair) ^ other
+        for sub in range(rows // ROWS):
+            tile = ((pair * 2 + half) * rows + sub * ROWS) // tile_rows
+            gates = jnp.zeros((ROWS, width), jnp.float32)
+            for column in range(tiles_w):
+                gates = jnp.where(lane == column, occupied[tile, column].astype(jnp.float32) * scale, gates)
+            span = pl.ds(sub * ROWS, ROWS)
+            for left in range(0, width, LANES):
+                lanes = pl.ds(left, LANES)
+                gate = gates[:, left : left + LANES]
+                total = jnp.zeros((ROWS, LANES), jnp.float32)
+                through = inverse = jnp.ones((ROWS, LANES), jnp.float32)
+                fore = [jnp.zeros((ROWS, LANES), jnp.float32) for _ in range(3)]
+                back = [jnp.zeros((ROWS, LANES), jnp.float32) for _ in range(3)]
+                for cell in range(depth_len):
+                    total = total + dense_buf[cell, pair, half, span, lanes]
+                    depth = total * gate
+                    through, last = jnp.exp2(depth), through
+                    inverse, last_inverse = jnp.exp2(-depth), inverse
+                    for channel in range(3):
+                        colour = emitted_buf[channel, cell, pair, half, span, lanes].astype(jnp.float32)
+                        fore[channel] = fore[channel] + colour * (last - through)
+                        back[channel] = back[channel] + colour * (inverse - last_inverse)
+                for channel in range(3):
+                    out[at, sub, channel, :, lanes] = fore[channel]
+                    out[at, sub, 4 + channel, :, lanes] = back[channel] * through
+                out[at, sub, 3, :, lanes] = through
+
+    for chunk in range(len(bounds) - 1):
         for copy in copies(chunk):
             copy.wait()
 
-        def march_pair(index, _):
-            pair = chunk * per + index
-            at = slot(pair, place, pairs) if ordered else pair
+        def march_pair(pair, _):
             for other, out in ((0, keep), (1, give)):
-                half = chosen ^ side(pair) ^ other
-                for sub in range(rows // ROWS):
-                    tile = ((pair * 2 + half) * rows + sub * ROWS) // tile_rows
-                    gate = jnp.zeros((ROWS, width), jnp.float32)
-                    for column in range(tiles_w):
-                        gate = jnp.where(lane == column, occupied[tile, column].astype(jnp.float32) * scale, gate)
-                    span = pl.ds(sub * ROWS, ROWS)
-                    total = jnp.zeros((ROWS, width), jnp.float32)
-                    before = jnp.ones((ROWS, width), jnp.float32)
-                    colour = [jnp.zeros((ROWS, width), jnp.float32) for _ in range(3)]
-                    for step in range(depth_len):
-                        cell = jnp.where(backward, depth_len - 1 - step, step)
-                        total = total + dense_buf[cell, pair, half, span, :]
-                        after = jnp.exp2(total * gate)
-                        weight = before - after
-                        before = after
-                        for channel in range(3):
-                            colour[channel] = colour[channel] + emitted_buf[channel, cell, pair, half, span, :].astype(jnp.float32) * weight
-                    for channel in range(3):
-                        out[at, sub, channel] = colour[channel]
-                    out[at, sub, 3] = before
+                march_tile(pair, other, out)
             return 0
 
-        lax.fori_loop(0, per, march_pair, 0)
-        return 0
-
-    lax.fori_loop(0, chunks, march_chunk, 0)
-
-
-def march(dense, emitted, occupied, facing, bricks, ordered):
+        lax.fori_loop(bounds[chunk], bounds[chunk + 1], march_pair, 0)
+
+
+def march(dense, emitted, occupied, bricks, ordered):
     _, pairs, _, rows, width = dense.shape
     tile_rows = pairs * 2 * rows // occupied.shape[0]
-    chunks = math.gcd(pairs, CHUNKS)
+    bounds = [pairs * eighth // 8 for eighth in BOUNDS] if pairs % 8 == 0 else [0, pairs]
+    chunks = len(bounds) - 1
     hbm = pl.BlockSpec(memory_space=pl.ANY)
-    half = pltpu.VMEM((pairs, rows // ROWS, 4, ROWS, width), jnp.float32)
+    half = pltpu.VMEM((pairs, rows // ROWS, 7, ROWS, width), jnp.float32)
     return pl.pallas_call(
-        functools.partial(march_body, chunks=chunks, tile_rows=tile_rows, bricks=bricks, ordered=ordered),
-        in_specs=[pl.BlockSpec(memory_space=pltpu.SMEM), hbm, hbm, hbm],
+        functools.partial(march_body, bounds=bounds, tile_rows=tile_rows, bricks=bricks, ordered=ordered),
+        in_specs=[hbm, hbm, hbm],
         out_specs=(pl.BlockSpec(memory_space=pltpu.VMEM), pl.BlockSpec(memory_space=pltpu.VMEM)),
         out_shape=(half, half),
         scratch_shapes=[
@@ -115,7 +120,7 @@
             pltpu.SemaphoreType.DMA,
         ],
         name="march",
-    )(facing, occupied, dense, emitted)
+    )(occupied, dense, emitted)
 
 
 def over(mine, other, nearer):
@@ -141,10 +146,15 @@
 
 def merge_cores(groups, nearer, arrays, outs):
     keep, got = arrays
+    forward = nearer(0)
+
+    def seen(tile):
+        return jnp.concatenate([jnp.where(forward, tile[:3], tile[4:]), tile[3:4]], axis=0)
+
     for group, out in zip(groups, outs):
         for k, at in enumerate(group):
             for sub in range(keep.shape[1]):
-                out[k, sub] = over(keep[at, sub], got[at, sub], nearer(1))
+                out[k, sub] = over(seen(keep[at, sub]), seen(got[at, sub]), nearer(1))
 
 
 def merge_square(bit, nearer, arrays, outs):
@@ -184,14 +194,14 @@
     dense = density.reshape(depth_len, pairs, 2, unit, width)
     emitted = emission.reshape(3, depth_len, pairs, 2, unit, width)
 
-    keep, give = march(dense, emitted, occupancy[0], facing, size, aligned)
+    keep, give = march(dense, emitted, occupancy[0], size, aligned)
     if not aligned:
         chosen = (place & 1) ^ side(place >> 1)
         pair = jnp.arange(pairs)
         swapped = ((chosen ^ side(pair)) == 1)[:, None, None, None]
         both = jnp.stack([jnp.where(swapped, give[:, 0], keep[:, 0]), jnp.where(swapped, keep[:, 0], give[:, 0])], axis=1)
         pairs = size // 2
-        both = jnp.moveaxis(both, 2, 0).reshape(4, pairs, 2, 1, rows, width)
+        both = jnp.moveaxis(both, 2, 0).reshape(7, pairs, 2, 1, rows, width)
         both = jnp.moveaxis(both, 0, 3)
         pair = jnp.arange(pairs)
         swapped = ((chosen ^ side(pair)) == 1)[:, None, None, None, None]
@@ -199,7 +209,7 @@
         keep = jnp.where(swapped, both[:, 1], both[:, 0])[order]
         give = jnp.where(swapped, both[:, 0], both[:, 1])[order]
     got = swap(give, 1, size)
-    tile = keep.shape[1:]
+    tile = (keep.shape[1], 4) + keep.shape[3:]
     quarter = pairs // 4
     later, sooner = list(range(0, quarter, 2)), list(range(1, quarter, 2))
     groups = {}

time: 18.8 us -> 18.7 us (level)
  waiting for transfers between devices: 4.3 us -> 3.93 us
  Pallas kernels: 3.49 us -> 3.8 us
    ppermute x7, waiting for transfers between devices: 4.3 us -> 3.93 us  [swap(): return lax.ppermute(value, 'depth', [(i, i ^ mask) for i in range(size)])]
    pallas_call x1, Pallas kernels: 2.77 us -> 3.06 us  [march(): pl.pallas_call(functools.partial(march_body, bounds=bounds, tile_rows=til...]
where the time goes in v6:
time: 18.7 us; the launch traced here: 18.6 us
  starting transfers between devices  10.2 us (55%)
  waiting for transfers between devices  3.93 us (21%)
  Pallas kernels  3.8 us (20%)
  between operations  0.69 us (4%)
    ppermute x7, starting transfers between devices, swap(): return lax.ppermute(value, 'depth', [(i, i ^ mask) for i in range(size)])  10.2 us
    ppermute x7, waiting for transfers between devices, swap(): return lax.ppermute(value, 'depth', [(i, i ^ mask) for i in range(size)])  3.93 us
    pallas_call x1, Pallas kernels, march(): pl.pallas_call(functools.partial(march_body, bounds=bounds, tile_rows=til...  3.06 us
    pallas_call x4, Pallas kernels, merge(): pl.pallas_call(kernel, in_specs=[pl.BlockSpec(memory_space=pltpu.SMEM)] +...  0.73 us
  transfers between devices with their start and end apart: 7, of which 3 were waited for; matrix products, arithmetic and copies ran while one was open for 0% of the time, Pallas kernels for 0%

profile of v6, /device:TPU:1, one launch (start us, length us, event | category | flops | bytes accessed | tf_op | source)
XLA Modules:
  0.0 18.6 jit_solution(11238849684627524093)
XLA Ops:
  0.0 3.1 %march.1 = (f32[8,1,7,8,256]{4,3,2,1,0:T(8,128)S(1)}, f32[8,1,7,8,256]{4,3,2,1,0:T(8,128)S(1)}) custom-call(s32[4,4]{1,0:T(4,128)} %bitcast.5, f32[16,8,2,8,256]{4,3,2,1,0:T(8,128)} %bitcast.4, bf16[3,16,8,2,8,256]{5,4,3,2,1,0:T(8,128)(2,1)} %bitcast.3), custom_call_target="tpu_custom_call" | custom-call | tf_op jit(solution)/shard_map/march/pallas_call | solution.py:109
  3.1 0.1 collective-permute-start
  3.8 1.1 %collective-permute-done.refs_1_ = f32[8,1,7,8,256]{4,3,2,1,0:T(8,128)S(1)} collective-permute-done((f32[8,1,7,8,256]{4,3,2,1,0:T(8,128)S(1)}, f32[8,1,7,8,256]{4,3,2,1,0:T(8,128)S(1)}, u32[]{:S(2)}, u32[]{:S(2)}) %collective-permute-start) | collective-permute-done | bytes 458784 | tf_op jit(solution)/shard_map/ppermute | solution.py:184
  5.0 0.1 shard_map.46
  5.0 3.7 %collective-permute-start.3 = (f32[2,1,4,8,256]{4,3,2,1,0:T(8,128)S(1)}, f32[2,1,4,8,256]{4,3,2,1,0:T(8,128)S(1)}, u32[]{:S(2)}, u32[]{:S(2)}) collective-permute-start(f32[2,1,4,8,256]{4,3,2,1,0:T(8,128)S(1)} %get-tuple-element.18), channel_id=1, source_target_pairs={{0,7},{1,6},{2,5},{3,4},{4,3},{5,2},{6,1},{7,0},{8,15},{9,14},{10,... | collective-permute-start | bytes 196616 | tf_op jit(solution)/shard_map/ppermute | solution.py:184
  8.7 0.2 %collective-permute-start.4 = (f32[1,1,4,8,256]{4,3,2,1,0:T(8,128)S(1)}, f32[1,1,4,8,256]{4,3,2,1,0:T(8,128)S(1)}, u32[]{:S(2)}, u32[]{:S(2)}) collective-permute-start(f32[1,1,4,8,256]{4,3,2,1,0:T(8,128)S(1)} %get-tuple-element.19), channel_id=1, source_target_pairs={{0,3},{1,2},{2,1},{3,0},{4,7},{5,6},{6,5},{7,4},{8,11},{9,10},{10,... | collective-permute-start | bytes 98312 | tf_op jit(solution)/shard_map/ppermute | solution.py:184
  9.0 0.1 collective-permute-start.5
  9.1 1.8 %collective-permute-start.1 = (f32[1,1,4,8,256]{4,3,2,1,0:T(8,128)S(1)}, f32[1,1,4,8,256]{4,3,2,1,0:T(8,128)S(1)}, u32[]{:S(2)}, u32[]{:S(2)}) collective-permute-start(f32[1,1,4,8,256]{4,3,2,1,0:T(8,128)S(1)} %get-tuple-element.16), channel_id=1, source_target_pairs={{0,3},{1,2},{2,1},{3,0},{4,7},{5,6},{6,5},{7,4},{8,11},{9,10},{10,... | collective-permute-start | bytes 98312 | tf_op jit(solution)/shard_map/ppermute | solution.py:184
  10.9 1.3 %collective-permute-start.2 = (f32[1,1,4,8,256]{4,3,2,1,0:T(8,128)S(1)}, f32[1,1,4,8,256]{4,3,2,1,0:T(8,128)S(1)}, u32[]{:S(2)}, u32[]{:S(2)}) collective-permute-start(f32[1,1,4,8,256]{4,3,2,1,0:T(8,128)S(1)} %get-tuple-element.17), channel_id=1, source_target_pairs={{0,4},{1,5},{2,6},{3,7},{4,0},{5,1},{6,2},{7,3},{8,12},{9,13},{10,... | collective-permute-start | bytes 98312 | tf_op jit(solution)/shard_map/ppermute | solution.py:184
  12.2 0.4 %collective-permute-done.4.refs_1_ = f32[1,1,4,8,256]{4,3,2,1,0:T(8,128)S(1)} collective-permute-done((f32[1,1,4,8,256]{4,3,2,1,0:T(8,128)S(1)}, f32[1,1,4,8,256]{4,3,2,1,0:T(8,128)S(1)}, u32[]{:S(2)}, u32[]{:S(2)}) %collective-permute-start.4) | collective-permute-done | bytes 32800 | tf_op jit(solution)/shard_map/ppermute | solution.py:184
  12.6 0.0 collective-permute-done.5.refs_2_
  12.6 0.0 collective-permute-done.3.refs_3_
  12.6 2.9 %collective-permute-start.6 = (f32[1,4,8,256]{3,2,1,0:T(8,128)S(1)}, f32[1,4,8,256]{3,2,1,0:T(8,128)S(1)}, u32[]{:S(2)}, u32[]{:S(2)}) collective-permute-start(f32[1,4,8,256]{3,2,1,0:T(8,128)S(1)} %shard_map.48), channel_id=1, source_target_pairs={{0,9},{1,8},{2,11},{3,10},{4,13},{5,12},{6,15},{7,14},{8,1},{9,0},... | collective-permute-start | bytes 98312 | tf_op jit(solution)/shard_map/ppermute | solution.py:184
  15.5 0.0 collective-permute-done.1.refs_1_
  15.5 0.0 collective-permute-done.2.refs_2_
  15.6 2.4 %collective-permute-done.6.refs_1_ = f32[1,4,8,256]{3,2,1,0:T(8,128)S(1)} collective-permute-done((f32[1,4,8,256]{3,2,1,0:T(8,128)S(1)}, f32[1,4,8,256]{3,2,1,0:T(8,128)S(1)}, u32[]{:S(2)}, u32[]{:S(2)}) %collective-permute-start.6) | collective-permute-done | bytes 32800 | tf_op jit(solution)/shard_map/ppermute | solution.py:184
  18.0 0.6 %shard_map.49 = f32[4,8,256]{2,1,0:T(8,128)} custom-call(s32[1]{0:T(128)S(6)} %copy.5.facing_ref, f32[1,4,8,256]{3,2,1,0:T(8,128)S(1)} %shard_map.47.refs_0_, f32[1,4,8,256]{3,2,1,0:T(8,128)S(1)} %collective-permute-done.6.refs_1_), custom_call_target="tpu_custom_call" | custom-call | tf_op jit(solution)/shard_map/pallas_call | solution.py:139
  (2 shorter events, 0.1 us)
Async XLA Ops:
  3.1 1.9 %collective-permute-start = (f32[8,1,7,8,256]{4,3,2,1,0:T(8,128)S(1)}, f32[8,1,7,8,256]{4,3,2,1,0:T(8,128)S(1)}, u32[]{:S(2)}, u32[]{:S(2)}) collective-permute-start(f32[8,1,7,8,256]{4,3,2,1,0:T(8,128)S(1)} %get-tuple-element.14), channel_id=1, source_target_pairs={{0,1},{1,0},{2,3},{3,2},{4,5},{5,4},{6,7},{7,6},{8,9},{9,8},{10,11... | collective-permute-start | bytes 1376264 | tf_op jit(solution)/shard_map/ppermute | solution.py:184
  5.0 7.6 %collective-permute-start.3 = (f32[2,1,4,8,256]{4,3,2,1,0:T(8,128)S(1)}, f32[2,1,4,8,256]{4,3,2,1,0:T(8,128)S(1)}, u32[]{:S(2)}, u32[]{:S(2)}) collective-permute-start(f32[2,1,4,8,256]{4,3,2,1,0:T(8,128)S(1)} %get-tuple-element.18), channel_id=1, source_target_pairs={{0,7},{1,6},{2,5},{3,4},{4,3},{5,2},{6,1},{7,0},{8,15},{9,14},{10,... | collective-permute-start | bytes 196616 | tf_op jit(solution)/shard_map/ppermute | solution.py:184
  8.7 3.9 %collective-permute-start.4 = (f32[1,1,4,8,256]{4,3,2,1,0:T(8,128)S(1)}, f32[1,1,4,8,256]{4,3,2,1,0:T(8,128)S(1)}, u32[]{:S(2)}, u32[]{:S(2)}) collective-permute-start(f32[1,1,4,8,256]{4,3,2,1,0:T(8,128)S(1)} %get-tuple-element.19), channel_id=1, source_target_pairs={{0,3},{1,2},{2,1},{3,0},{4,7},{5,6},{6,5},{7,4},{8,11},{9,10},{10,... | collective-permute-start | bytes 98312 | tf_op jit(solution)/shard_map/ppermute | solution.py:184
  9.0 3.6 %collective-permute-start.5 = (f32[1,1,4,8,256]{4,3,2,1,0:T(8,128)S(1)}, f32[1,1,4,8,256]{4,3,2,1,0:T(8,128)S(1)}, u32[]{:S(2)}, u32[]{:S(2)}) collective-permute-start(f32[1,1,4,8,256]{4,3,2,1,0:T(8,128)S(1)} %get-tuple-element.20), channel_id=1, source_target_pairs={{0,4},{1,5},{2,6},{3,7},{4,0},{5,1},{6,2},{7,3},{8,12},{9,13},{10,... | collective-permute-start | bytes 98312 | tf_op jit(solution)/shard_map/ppermute | solution.py:184
  9.1 6.5 %collective-permute-start.1 = (f32[1,1,4,8,256]{4,3,2,1,0:T(8,128)S(1)}, f32[1,1,4,8,256]{4,3,2,1,0:T(8,128)S(1)}, u32[]{:S(2)}, u32[]{:S(2)}) collective-permute-start(f32[1,1,4,8,256]{4,3,2,1,0:T(8,128)S(1)} %get-tuple-element.16), channel_id=1, source_target_pairs={{0,3},{1,2},{2,1},{3,0},{4,7},{5,6},{6,5},{7,4},{8,11},{9,10},{10,... | collective-permute-start | bytes 98312 | tf_op jit(solution)/shard_map/ppermute | solution.py:184
  10.9 4.6 %collective-permute-start.2 = (f32[1,1,4,8,256]{4,3,2,1,0:T(8,128)S(1)}, f32[1,1,4,8,256]{4,3,2,1,0:T(8,128)S(1)}, u32[]{:S(2)}, u32[]{:S(2)}) collective-permute-start(f32[1,1,4,8,256]{4,3,2,1,0:T(8,128)S(1)} %get-tuple-element.17), channel_id=1, source_target_pairs={{0,4},{1,5},{2,6},{3,7},{4,0},{5,1},{6,2},{7,3},{8,12},{9,13},{10,... | collective-permute-start | bytes 98312 | tf_op jit(solution)/shard_map/ppermute | solution.py:184
  12.6 5.3 %collective-permute-start.6 = (f32[1,4,8,256]{3,2,1,0:T(8,128)S(1)}, f32[1,4,8,256]{3,2,1,0:T(8,128)S(1)}, u32[]{:S(2)}, u32[]{:S(2)}) collective-permute-start(f32[1,4,8,256]{3,2,1,0:T(8,128)S(1)} %shard_map.48), channel_id=1, source_target_pairs={{0,9},{1,8},{2,11},{3,10},{4,13},{5,12},{6,15},{7,14},{8,1},{9,0},... | collective-permute-start | bytes 98312 | tf_op jit(solution)/shard_map/ppermute | solution.py:184
